TPU v7x, 256 devices: a whole 4x4x8 slice. The times are simulated.
256 devices in a mesh: ha: 64 (over y_lo, z, x), ta: 4 (over y_hi, core).
Axes of the slice: x: 4, y: 4 (y_hi: 2, y_lo: 2; y = y_hi * 2 + y_lo), z: 8, core: 2. Of those that a mesh axis runs over, the one named last changes fastest.
Arguments:
- layer_input: bfloat16 [8, 192, 192, 128], P('ta', 'ha'), may hold values from -6 to 6
- pre_one: bfloat16 [8, 192, 192, 128], P('ta', 'ha'), may hold values from -9 to 9
- pre_two: bfloat16 [8, 192, 192, 128], P('ta', 'ha'), may hold values from -9 to 9
- pre_three: bfloat16 [8, 192, 192, 128], P('ta', 'ha'), may hold values from -9 to 9
- kernel_one: bfloat16 [3, 3, 3, 128, 128], replicated, may hold values from -0.109375 to 0.109375
- kernel_two: bfloat16 [3, 3, 3, 128, 128], replicated, may hold values from -0.109375 to 0.109375
- kernel_three: bfloat16 [3, 3, 3, 128, 128], replicated, may hold values from -0.109375 to 0.109375
- upstream: bfloat16 [8, 192, 192, 128], P('ta', 'ha'), may hold values from -24 to 24
Outputs:
- input_gradient: bfloat16 [8, 192, 192, 128], P('ta', 'ha')
- kernel_grad_one: float32 [3, 3, 3, 128, 128], P(None, None, None, 'ha')
- kernel_grad_two: float32 [3, 3, 3, 128, 128], P(None, None, None, 'ha')
- kernel_grad_three: float32 [3, 3, 3, 128, 128], P(None, None, None, 'ha')
All inputs are finite; a program needn't handle non-finite values.
Results may differ from a plain program's by a relative error of at most 0.014.
Values may be sent and summed in bfloat16 or wider, within the bound.
No kernel may reach another device: no remote copies, remote signals or barrier semaphores. Data moves between devices by JAX's collectives and lax.ppermute only.
A program may use at most 128 MiB of HBM per device.

v0:
```python
import math

import jax
import jax.numpy as jnp
from jax import lax
from jax.sharding import PartitionSpec as P


def from_behind(block, axis, distance):
    devices = range(lax.axis_size(axis))
    route = [(i - distance, i) for i in devices if i - distance in devices]
    return lax.ppermute(block, axis, route)


def padded(x, sides, width):
    for axis, dim in sides:
        peers, length = (lax.axis_size(axis), x.shape[dim])
        up = [(i, (i + 1) % peers) for i in range(peers - 1)]
        down = [(j, i) for i, j in up]
        last = lax.slice_in_dim(x, length - width, length, axis=dim)
        initial = lax.slice_in_dim(x, 0, width, axis=dim)
        before = lax.ppermute(last, axis, up)
        after = lax.ppermute(initial, axis, down)
        x = jnp.concatenate([before, x, after], axis=dim)
    return x


def together(arrays, axis):
    ends = [0]
    for a in arrays:
        ends.append(ends[-1] + a.size)
    subtotal = lax.psum(jnp.concatenate([a.ravel() for a in arrays]), axis)
    return tuple((subtotal[b:e].reshape(a.shape) for a, b, e in zip(arrays, ends, ends[1:])))


def silu_slope(pre_values):
    values = pre_values.astype(jnp.float32)
    sigmoid = jax.nn.sigmoid(values)
    return sigmoid * (1.0 + values * (1.0 - sigmoid))


def forward_taps(widened, frame_count, row_count, col_count):
    tap_list = [
        widened[
            tap_time : tap_time + frame_count,
            tap_row : tap_row + row_count,
            tap_col : tap_col + col_count,
        ]
        for tap_time in range(3)
        for tap_row in range(3)
        for tap_col in range(3)
    ]
    patches = jnp.concatenate(tap_list, -1)
    return patches.reshape(-1, patches.shape[-1])


def gather_grad(gradient, kernel):
    frame_count, row_count, col_count, channels = gradient.shape
    ahead = from_behind(gradient, "ta", -1)
    joined = jnp.concatenate([gradient, ahead], 0)
    rimmed = padded(joined, (("ha", 1),), 1)
    widened = jnp.pad(rimmed, ((0, 0), (0, 0), (1, 1), (0, 0)))
    tap_list = [
        widened[
            2 - tap_time : 2 - tap_time + frame_count,
            2 - tap_row : 2 - tap_row + row_count,
            2 - tap_col : 2 - tap_col + col_count,
        ]
        for tap_time in range(3)
        for tap_row in range(3)
        for tap_col in range(3)
    ]
    patches = jnp.concatenate(tap_list, -1).reshape(-1, 27 * channels)
    flipped = jnp.swapaxes(kernel, 3, 4).reshape(27 * channels, channels)
    result = jnp.dot(patches, flipped, preferred_element_type=jnp.float32)
    return result.reshape(frame_count, row_count, col_count, channels)


def input_grad(gradient, kernel):
    return gather_grad(gradient, kernel)


def own_block(full_term, channels, piece_width):
    shaped = full_term.reshape(3, 3, 3, channels, channels)
    return lax.dynamic_slice_in_dim(shaped, lax.axis_index("ha") * piece_width, piece_width, 3)


def shards(
    layer_input, pre_one, pre_two, pre_three, kernel_one, kernel_two, kernel_three, upstream
):
    frame_count, row_count, col_count, channels = layer_input.shape
    piece_width = channels // lax.axis_size("ha")
    cells_total = frame_count * row_count * col_count * lax.axis_size("ta") * lax.axis_size("ha")
    norm_scale = 1.0 / math.sqrt(cells_total)
    act_one = jax.nn.silu(pre_one.astype(jnp.float32)).astype(jnp.bfloat16)
    act_two = jax.nn.silu(pre_two.astype(jnp.float32)).astype(jnp.bfloat16)
    stacked = jnp.stack([layer_input, act_one, act_two], 0)
    earlier = from_behind(stacked, "ta", 1)
    joined = jnp.concatenate([earlier, stacked], 1)
    rimmed = padded(joined, (("ha", 2),), 1)
    widened = jnp.pad(rimmed, ((0, 0), (0, 0), (0, 0), (1, 1), (0, 0)))
    gradient = (upstream.astype(jnp.float32) * silu_slope(pre_three)).astype(jnp.bfloat16)
    layer_list = [(kernel_three, pre_two, 2), (kernel_two, pre_one, 1), (kernel_one, None, 0)]
    pending = []
    reduced = []
    input_gradient = None
    for kernel, previous, depth_index in layer_list:
        patches = forward_taps(widened[depth_index], frame_count, row_count, col_count)
        grad_flat = gradient.reshape(-1, channels)
        pending.append(
            lax.dot_general(
                patches, grad_flat, (((0,), (0,)), ((), ())), preferred_element_type=jnp.float32
            )
        )
        back_grad = input_grad(gradient, kernel)
        if previous is None:
            input_gradient = back_grad.astype(jnp.bfloat16)
        else:
            gradient = (back_grad * silu_slope(previous)).astype(jnp.bfloat16)
    summed = together((pending[0], pending[1], pending[2]), ("ha", "ta"))
    reduced = [own_block(entry, channels, piece_width) * norm_scale for entry in summed]
    return (input_gradient, reduced[2], reduced[1], reduced[0])


def solution(mesh):
    return jax.shard_map(
        shards,
        mesh=mesh,
        in_specs=(
            P("ta", "ha", None, None),
            P("ta", "ha", None, None),
            P("ta", "ha", None, None),
            P("ta", "ha", None, None),
            P(),
            P(),
            P(),
            P("ta", "ha", None, None),
        ),
        out_specs=(
            P("ta", "ha", None, None),
            P(None, None, None, "ha", None),
            P(None, None, None, "ha", None),
            P(None, None, None, "ha", None),
        ),
        check_vma=False,
    )
```

profile of v0, /device:TPU:97, one launch (start us, length us, event | category | flops | bytes accessed | tf_op | source)
XLA Modules:
  0.0 404.9 jit_solution(12086418513729050629)
XLA Ops:
  7.2 1.3 fusion.34
  8.5 2.6 collective-permute-start
  12.2 6.1 %collective-permute-done = bf16[2,3,192,128]{3,2,1,0:T(8,128)(2,1)S(1)} collective-permute-done((bf16[2,3,192,128]{3,2,1,0:T(8,128)(2,1)S(1)}, bf16[2,3,192,128]{3,2,1,0:T(8,128)(2,1)S(1)}, u32[]{:S(2)}, u32[]{:S(2)}) %collective-permute-start) | collective-permute-done | bytes 294944 | tf_op jit(solution)/shard_map/ppermute | solution.py:12
  18.3 3.1 collective-permute-start.1
  21.5 4.3 %collective-permute-start.2 = (bf16[4,1,192,128]{3,2,1,0:T(8,128)(2,1)S(1)}, bf16[4,1,192,128]{3,2,1,0:T(8,128)(2,1)S(1)}, u32[]{:S(2)}, u32[]{:S(2)}) collective-permute-start(bf16[4,1,192,128]{3,2,1,0:T(8,128)(2,1)S(1)} %get-tuple-element.23), channel_id=1, source_target_pairs={{4,0},{8,4},{12,8},{16,12},{20,16},{24,20},{28,24},{32,28},{36,32}... | collective-permute-start | bytes 589832 | tf_op jit(solution)/shard_map/ppermute | solution.py:23
  25.7 1.1 fusion.48
  26.9 2.0 pad_maximum_fusion.1
  28.9 2.3 collective-permute-start.9
  31.2 2.3 copy.12
  36.5 2.3 fusion.9
  38.8 2.1 collective-permute-start.3
  40.9 7.5 %collective-permute-done.3 = bf16[2,3,192,128]{3,2,1,0:T(8,128)(2,1)S(1)} collective-permute-done((bf16[2,3,192,128]{3,2,1,0:T(8,128)(2,1)S(1)}, bf16[2,3,192,128]{3,2,1,0:T(8,128)(2,1)S(1)}, u32[]{:S(2)}, u32[]{:S(2)}) %collective-permute-start.3) | collective-permute-done | bytes 294944 | tf_op jit(solution)/shard_map/ppermute | solution.py:12
  48.4 1.9 collective-permute-start.4
  50.3 5.5 %collective-permute-start.5 = (bf16[4,1,192,128]{3,2,1,0:T(8,128)(2,1)S(1)}, bf16[4,1,192,128]{3,2,1,0:T(8,128)(2,1)S(1)}, u32[]{:S(2)}, u32[]{:S(2)}) collective-permute-start(bf16[4,1,192,128]{3,2,1,0:T(8,128)(2,1)S(1)} %get-tuple-element.19), channel_id=1, source_target_pairs={{4,0},{8,4},{12,8},{16,12},{20,16},{24,20},{28,24},{32,28},{36,32}... | collective-permute-start | bytes 589832 | tf_op jit(solution)/shard_map/ppermute | solution.py:23
  55.8 2.3 copy.13
  58.1 1.2 pad_maximum_fusion.8
  59.2 1.9 collective-permute-start.10
  61.2 5.5 %collective-permute-start.11 = (bf16[3,4,1,192,128]{4,3,2,1,0:T(8,128)(2,1)}, bf16[3,4,1,192,128]{4,3,2,1,0:T(8,128)(2,1)}, u32[]{:S(2)}, u32[]{:S(2)}) collective-permute-start(bf16[3,4,1,192,128]{4,3,2,1,0:T(8,128)(2,1)} %get-tuple-element.11), channel_id=1, source_target_pairs={{4,0},{8,4},{12,8},{16,12},{20,16},{24,20},{28,24},{32,28},{36,32}... | collective-permute-start | bytes 1769480 | tf_op jit(solution)/shard_map/ppermute | solution.py:23
  69.7 2.3 fusion.10
  72.0 1.9 collective-permute-start.6
  73.9 2.3 copy.14
  76.2 5.3 %collective-permute-done.6 = bf16[2,3,192,128]{3,2,1,0:T(8,128)(2,1)S(1)} collective-permute-done((bf16[2,3,192,128]{3,2,1,0:T(8,128)(2,1)S(1)}, bf16[2,3,192,128]{3,2,1,0:T(8,128)(2,1)S(1)}, u32[]{:S(2)}, u32[]{:S(2)}) %collective-permute-start.6) | collective-permute-done | bytes 294944 | tf_op jit(solution)/shard_map/ppermute | solution.py:12
  82.2 1.9 collective-permute-start.7
  84.1 5.5 %collective-permute-start.8 = (bf16[4,1,192,128]{3,2,1,0:T(8,128)(2,1)S(1)}, bf16[4,1,192,128]{3,2,1,0:T(8,128)(2,1)S(1)}, u32[]{:S(2)}, u32[]{:S(2)}) collective-permute-start(bf16[4,1,192,128]{3,2,1,0:T(8,128)(2,1)S(1)} %get-tuple-element.15), channel_id=1, source_target_pairs={{4,0},{8,4},{12,8},{16,12},{20,16},{24,20},{28,24},{32,28},{36,32}... | collective-permute-start | bytes 589832 | tf_op jit(solution)/shard_map/ppermute | solution.py:23
  89.6 3.9 select_maximum_fusion
  99.8 2.3 convolution_bitcast_fusion.2
  102.1 2.3 convolution_bitcast_fusion.1
  107.7 2.3 convolution_bitcast_fusion
  110.0 6.3 %pad_maximum_fusion = f32[1327104]{0:T(1024)} fusion(f32[442368]{0:T(1024)S(1)} %convolution_bitcast_fusion, f32[442368]{0:T(1024)S(1)} %convolution_bitcast_fusion.1, f32[442368]{0:T(1024)S(1)} %convolution_bitcast_fusion.2), kind=kLoop, calls=%fused_computation.6 | loop fusion | flops 2654208 | bytes 10616832 | tf_op jit(solution)/shard_map/concatenate | solution.py:32
  119.3 2.9 convolution_convert_fusion
  122.3 271.0 %all-reduce.6.cloned.1.call-done = f32[1327104]{0:T(1024)} async-done(((f32[1327104]{0:T(1024)}), f32[1327104]{0:T(1024)}) %all-reduce.6.cloned.1.call-update) | async-done | bytes 5308432 | tf_op jit(solution)/shard_map/psum | solution.py:32
  393.3 2.9 fusion.55
  (198 shorter events, 21.1 us)
Async XLA Ops:
  7.2 386.2 %all-reduce.6.cloned.1.call-start = ((), (), s32[]{:S(2)}) async-start(), calls=%async_computation | async-start | bytes 10616832 | tf_op jit(solution)/shard_map/psum | solution.py:32
  8.5 9.8 %collective-permute-start = (bf16[2,3,192,128]{3,2,1,0:T(8,128)(2,1)S(1)}, bf16[2,3,192,128]{3,2,1,0:T(8,128)(2,1)S(1)}, u32[]{:S(2)}, u32[]{:S(2)}) collective-permute-start(bf16[2,3,192,128]{3,2,1,0:T(8,128)(2,1)S(1)} %fusion.34), channel_id=1, source_target_pairs={{1,0},{2,1},{3,2},{5,4},{6,5},{7,6},{9,8},{10,9},{11,10},{13,12},{... | collective-permute-start | bytes 884744 | tf_op jit(solution)/shard_map/ppermute | solution.py:12
  18.3 15.2 %collective-permute-start.1 = (bf16[4,1,192,128]{3,2,1,0:T(8,128)(2,1)S(1)}, bf16[4,1,192,128]{3,2,1,0:T(8,128)(2,1)S(1)}, u32[]{:S(2)}, u32[]{:S(2)}) collective-permute-start(bf16[4,1,192,128]{3,2,1,0:T(8,128)(2,1)S(1)} %get-tuple-element.22), channel_id=1, source_target_pairs={{0,4},{4,8},{8,12},{12,16},{16,20},{20,24},{24,28},{28,32},{32,36}... | collective-permute-start | bytes 589832 | tf_op jit(solution)/shard_map/ppermute | solution.py:22
  21.5 12.0 %collective-permute-start.2 = (bf16[4,1,192,128]{3,2,1,0:T(8,128)(2,1)S(1)}, bf16[4,1,192,128]{3,2,1,0:T(8,128)(2,1)S(1)}, u32[]{:S(2)}, u32[]{:S(2)}) collective-permute-start(bf16[4,1,192,128]{3,2,1,0:T(8,128)(2,1)S(1)} %get-tuple-element.23), channel_id=1, source_target_pairs={{4,0},{8,4},{12,8},{16,12},{20,16},{24,20},{28,24},{32,28},{36,32}... | collective-permute-start | bytes 589832 | tf_op jit(solution)/shard_map/ppermute | solution.py:23
  28.9 29.2 %collective-permute-start.9 = (bf16[3,2,3,192,128]{4,3,2,1,0:T(8,128)(2,1)}, bf16[3,2,3,192,128]{4,3,2,1,0:T(8,128)(2,1)S(1)}, u32[]{:S(2)}, u32[]{:S(2)}) collective-permute-start(bf16[3,2,3,192,128]{4,3,2,1,0:T(8,128)(2,1)} %pad_maximum_fusion.1), channel_id=1, source_target_pairs={{0,1},{1,2},{2,3},{4,5},{5,6},{6,7},{8,9},{9,10},{10,11},{12,13},{... | collective-permute-start | bytes 2654216 | tf_op jit(solution)/shard_map/ppermute | solution.py:12
  34.0 2.5 copy-start.3
  34.0 2.5 copy-start.4
  36.5 21.6 %copy-start = (bf16[2,3,192,128]{3,2,1,0:T(8,128)(2,1)S(1)}, bf16[2,3,192,128]{3,2,1,0:T(8,128)(2,1)}, u32[]{:S(2)}) copy-start(bf16[2,3,192,128]{3,2,1,0:T(8,128)(2,1)} %param.8) | copy-start | bytes 884740
  38.8 9.5 %collective-permute-start.3 = (bf16[2,3,192,128]{3,2,1,0:T(8,128)(2,1)S(1)}, bf16[2,3,192,128]{3,2,1,0:T(8,128)(2,1)S(1)}, u32[]{:S(2)}, u32[]{:S(2)}) collective-permute-start(bf16[2,3,192,128]{3,2,1,0:T(8,128)(2,1)S(1)} %fusion.9), channel_id=1, source_target_pairs={{1,0},{2,1},{3,2},{5,4},{6,5},{7,6},{9,8},{10,9},{11,10},{13,12},{... | collective-permute-start | bytes 884744 | tf_op jit(solution)/shard_map/ppermute | solution.py:12
  48.4 18.3 %collective-permute-start.4 = (bf16[4,1,192,128]{3,2,1,0:T(8,128)(2,1)S(1)}, bf16[4,1,192,128]{3,2,1,0:T(8,128)(2,1)S(1)}, u32[]{:S(2)}, u32[]{:S(2)}) collective-permute-start(bf16[4,1,192,128]{3,2,1,0:T(8,128)(2,1)S(1)} %get-tuple-element.18), channel_id=1, source_target_pairs={{0,4},{4,8},{8,12},{12,16},{16,20},{20,24},{24,28},{28,32},{32,36}... | collective-permute-start | bytes 589832 | tf_op jit(solution)/shard_map/ppermute | solution.py:22
  50.3 16.3 %collective-permute-start.5 = (bf16[4,1,192,128]{3,2,1,0:T(8,128)(2,1)S(1)}, bf16[4,1,192,128]{3,2,1,0:T(8,128)(2,1)S(1)}, u32[]{:S(2)}, u32[]{:S(2)}) collective-permute-start(bf16[4,1,192,128]{3,2,1,0:T(8,128)(2,1)S(1)} %get-tuple-element.19), channel_id=1, source_target_pairs={{4,0},{8,4},{12,8},{16,12},{20,16},{24,20},{28,24},{32,28},{36,32}... | collective-permute-start | bytes 589832 | tf_op jit(solution)/shard_map/ppermute | solution.py:23
  59.2 30.4 %collective-permute-start.10 = (bf16[3,4,1,192,128]{4,3,2,1,0:T(8,128)(2,1)}, bf16[3,4,1,192,128]{4,3,2,1,0:T(8,128)(2,1)}, u32[]{:S(2)}, u32[]{:S(2)}) collective-permute-start(bf16[3,4,1,192,128]{4,3,2,1,0:T(8,128)(2,1)} %get-tuple-element.10), channel_id=1, source_target_pairs={{0,4},{4,8},{8,12},{12,16},{16,20},{20,24},{24,28},{28,32},{32,36}... | collective-permute-start | bytes 1769480 | tf_op jit(solution)/shard_map/ppermute | solution.py:22
  61.2 28.5 %collective-permute-start.11 = (bf16[3,4,1,192,128]{4,3,2,1,0:T(8,128)(2,1)}, bf16[3,4,1,192,128]{4,3,2,1,0:T(8,128)(2,1)}, u32[]{:S(2)}, u32[]{:S(2)}) collective-permute-start(bf16[3,4,1,192,128]{4,3,2,1,0:T(8,128)(2,1)} %get-tuple-element.11), channel_id=1, source_target_pairs={{4,0},{8,4},{12,8},{16,12},{20,16},{24,20},{28,24},{32,28},{36,32}... | collective-permute-start | bytes 1769480 | tf_op jit(solution)/shard_map/ppermute | solution.py:23
  67.2 2.5 copy-start.2
  67.2 2.5 copy-start.5
  72.0 9.5 %collective-permute-start.6 = (bf16[2,3,192,128]{3,2,1,0:T(8,128)(2,1)S(1)}, bf16[2,3,192,128]{3,2,1,0:T(8,128)(2,1)S(1)}, u32[]{:S(2)}, u32[]{:S(2)}) collective-permute-start(bf16[2,3,192,128]{3,2,1,0:T(8,128)(2,1)S(1)} %fusion.10), channel_id=1, source_target_pairs={{1,0},{2,1},{3,2},{5,4},{6,5},{7,6},{9,8},{10,9},{11,10},{13,12},{... | collective-permute-start | bytes 884744 | tf_op jit(solution)/shard_map/ppermute | solution.py:12
  82.2 34.1 %collective-permute-start.7 = (bf16[4,1,192,128]{3,2,1,0:T(8,128)(2,1)}, bf16[4,1,192,128]{3,2,1,0:T(8,128)(2,1)S(1)}, u32[]{:S(2)}, u32[]{:S(2)}) collective-permute-start(bf16[4,1,192,128]{3,2,1,0:T(8,128)(2,1)} %get-tuple-element.14), channel_id=1, source_target_pairs={{0,4},{4,8},{8,12},{12,16},{16,20},{20,24},{24,28},{28,32},{32,36}... | collective-permute-start | bytes 589832 | tf_op jit(solution)/shard_map/ppermute | solution.py:22
  84.1 32.2 %collective-permute-start.8 = (bf16[4,1,192,128]{3,2,1,0:T(8,128)(2,1)S(1)}, bf16[4,1,192,128]{3,2,1,0:T(8,128)(2,1)S(1)}, u32[]{:S(2)}, u32[]{:S(2)}) collective-permute-start(bf16[4,1,192,128]{3,2,1,0:T(8,128)(2,1)S(1)} %get-tuple-element.15), channel_id=1, source_target_pairs={{4,0},{8,4},{12,8},{16,12},{20,16},{24,20},{28,24},{32,28},{36,32}... | collective-permute-start | bytes 589832 | tf_op jit(solution)/shard_map/ppermute | solution.py:23
  116.9 2.5 copy-start.1
Sparse Core Ops, SparseCore 0:
  116.5 276.8 all-reduce.5
where the time goes:
time: 406 us; the launch traced here: 405 us
  waiting for transfers between devices  290 us (71%)
  starting transfers between devices  38.5 us (9%)
  local copies, waits for them, and re-layouts  25.6 us (6%)
  other arithmetic  21 us (5%)
  between operations  15.6 us (4%)
  matrix products  14.4 us (4%)
    psum x1, waiting for transfers between devices, together(): subtotal = lax.psum(jnp.concatenate([a.ravel() for a in arrays]), axis)  271 us
    unnamed x168, local copies, waits for them, and re-layouts  21.9 us
    ppermute x4, starting transfers between devices, padded(): after = lax.ppermute(initial, axis, down)  20.7 us
    ppermute x4, waiting for transfers between devices, from_behind(): return lax.ppermute(block, axis, route)  18.9 us
    ppermute x4, starting transfers between devices, from_behind(): return lax.ppermute(block, axis, route)  8.87 us
    ppermute x4, starting transfers between devices, padded(): before = lax.ppermute(last, axis, up)  8.86 us
  transfers between devices with their start and end apart: 13, of which 4 were waited for; matrix products, arithmetic and copies ran while one was open for 14% of the time, Pallas kernels for 0%

commit v1 on v0

v1 whole, which is shorter than its diff:
```python
import functools
import math

import jax
import jax.numpy as jnp
from jax import lax
from jax.experimental import pallas as pl
from jax.experimental.pallas import tpu as pltpu
from jax.sharding import PartitionSpec as P


HALO = 8
OUTSIDE = -1000.0
TAPS = 27
SLOTS = 32
MIB = 1024 * 1024
LIMIT = 18
VMEM = pl.BlockSpec(memory_space=pltpu.VMEM)
SMEM = pl.BlockSpec(memory_space=pltpu.SMEM)
GROUPS = ((0, 1), (2, 3), (4, 5), (6, 7), (8,))


def call(body, out_shape, operands, flops, scratch=(), scalar=None):
    moved = sum(a.size * a.dtype.itemsize for a in operands)
    moved += sum(math.prod(s.shape) * s.dtype.itemsize for s in out_shape)
    count, results = len(operands), len(out_shape)
    skip = 0 if scalar is None else 1

    def kernel(*refs):
        loaded = refs[skip : skip + count]
        rest = refs[skip + count :]
        body(*refs[:skip], loaded, rest[:results], *rest[results:])

    return pl.pallas_call(
        kernel,
        out_shape=tuple(out_shape),
        in_specs=[SMEM] * skip + [VMEM] * count,
        out_specs=(VMEM,) * results,
        scratch_shapes=list(scratch),
        compiler_params=pltpu.CompilerParams(vmem_limit_bytes=LIMIT * MIB),
        cost_estimate=pl.CostEstimate(flops=flops, bytes_accessed=moved, transcendentals=0),
    )(*([] if scalar is None else [scalar]), *operands)


def slope(pre_values):
    values = pre_values.astype(jnp.float32)
    sigmoid = jax.nn.sigmoid(values)
    return sigmoid * (1.0 + values * (1.0 - sigmoid))


def silu(pre_values):
    values = pre_values.astype(jnp.float32)
    return (values * jax.nn.sigmoid(values)).astype(jnp.bfloat16)


def split_columns(value, out_ref, outside):
    parts, own = out_ref.shape[0], out_ref.shape[3] - 2 * HALO
    shape = value.shape[:2] + (2 * HALO, value.shape[3])
    fill = jnp.full(shape, outside, value.dtype)
    first = lax.broadcasted_iota(jnp.int32, shape, 2) < HALO
    for part in range(parts):
        begin, end = part * own, (part + 1) * own
        out_ref[part, :, :, 0:own] = value[:, :, begin:end]
        right = value[:, :, end : end + 2 * HALO] if part < parts - 1 else fill
        left = value[:, :, begin - 2 * HALO : begin] if part else fill
        tail = jnp.where(first, right.astype(jnp.float32), left.astype(jnp.float32))
        out_ref[part, :, :, own : own + 2 * HALO] = tail.astype(value.dtype)


def split_first(loaded, outs):
    upstream, pre, two = loaded
    (out_ref,) = outs
    wide = out_ref.shape[3] // 2
    upstream_ref, pre_ref = upstream, pre
    gradient = upstream_ref[...].astype(jnp.float32) * slope(pre_ref[...])
    split_columns(gradient.astype(jnp.bfloat16), out_ref.at[:, :, :, 0:wide], 0.0)
    split_columns(two[...], out_ref.at[:, :, :, wide : 2 * wide], OUTSIDE)


def split_second(loaded, outs):
    (out_ref,) = outs
    one_ref, input_ref = loaded[0], loaded[1]
    parts = out_ref.shape[0]
    own = input_ref.shape[2] // parts
    wide = own + 2 * HALO
    split_columns(one_ref[...], out_ref.at[:, :, :, 0:wide], OUTSIDE)
    for part in range(parts):
        out_ref[part, :, :, wide : wide + own] = input_ref[:, :, part * own : (part + 1) * own]


def fill_window(own, before, after, window_ref):
    own_ref, before_ref, after_ref = own, before, after
    frames, rows, channels = own_ref.shape[0], own_ref.shape[1], own_ref.shape[3]
    cols = before_ref.shape[1]
    window_ref[frames : frames + 2] = jnp.zeros((2,) + window_ref.shape[1:], window_ref.dtype)
    for frame in range(frames):
        sources = [before_ref[frame]] + [own_ref[frame, r, 0:cols] for r in range(rows)] + [after_ref[frame]]
        for r, block in enumerate(sources):
            wide = block.astype(jnp.float32)
            following = pltpu.roll(wide, cols - 1, 0).astype(window_ref.dtype)
            preceding = pltpu.roll(wide, 1, 0).astype(window_ref.dtype)
            window_ref[frame, r, :, 0:channels] = following
            window_ref[frame, r, :, channels : 2 * channels] = block
            window_ref[frame, r, :, 2 * channels : 3 * channels] = preceding


def input_grad_kernel(loaded, outs, window_ref, *, begin):
    own, before, after, kernel, *pre = loaded
    frames, rows, channels = own.shape[0], own.shape[1], own.shape[3]
    cols = before.shape[1]
    out_ref, width = outs[0], outs[0].shape[2]
    fill_window(own, before, after, window_ref)
    kernel_ref = kernel
    if pre:
        pre_ref = pre[0]
        first_ref, final_ref = outs[1:]
    weights = []
    for group in GROUPS:
        weights.append(
            jnp.concatenate([kernel_ref[3 * pair + c] for pair in group for c in range(3)], -1)
        )
    step = 2
    for f in range(0, frames, step):
        total = None
        for group, weight in zip(GROUPS, weights):
            pieces = []
            for pair in group:
                a, b = divmod(pair, 3)
                block = window_ref[f + 2 - a : f + 2 - a + step, 2 - b : 2 - b + rows, 0:width]
                pieces.append(block.reshape(step * rows * width, 3 * channels))
            patches = jnp.concatenate(pieces, -1) if len(pieces) > 1 else pieces[0]
            term = lax.dot_general(
                patches, weight, (((1,), (1,)), ((), ())), preferred_element_type=jnp.float32
            )
            total = term if total is None else total + term
        total = total.reshape(step, rows, width, channels)
        if not pre:
            out_ref[f : f + step] = total.astype(jnp.bfloat16)
        else:
            result = (total * slope(pre_ref[f : f + step, :, begin : begin + cols])).astype(jnp.bfloat16)
            out_ref[f : f + step] = result
            first_ref[f : f + step] = result[:, 0]
            final_ref[f : f + step] = result[:, rows - 1]


def kernel_grad_kernel(half_ref, loaded, outs, window_ref, spread_ref, *, activate, width, begin):
    own, before, after, kept = loaded
    keep_ref, send_ref = outs
    frames, rows, channels = own.shape[0], own.shape[1], own.shape[3]
    cells = frames * rows * width
    half = channels // 2
    fill_window(own, before, after, window_ref)
    saved = kept[:, :, begin : begin + width]
    if activate:
        saved = silu(saved)
    left = saved.reshape(cells, channels).T
    spread_ref[...] = jnp.zeros(spread_ref.shape, spread_ref.dtype)
    for pair in range(9):
        a, b = divmod(pair, 3)
        block = window_ref[2 - a : 2 - a + frames, 2 - b : 2 - b + rows, 0:width]
        term = jnp.dot(
            left, block.reshape(cells, 3 * channels), preferred_element_type=jnp.float32
        )
        for c in range(3):
            spread_ref[pl.ds(3 * pair + c, channels, stride=SLOTS), :] = term[
                :, c * channels : (c + 1) * channels
            ]
    paired = spread_ref.reshape(half, 2 * SLOTS, channels)
    mine = pl.multiple_of(half_ref[0] * SLOTS, SLOTS)
    other = pl.multiple_of((1 - half_ref[0]) * SLOTS, SLOTS)
    keep_ref[...] = paired[:, pl.ds(mine, SLOTS), :]
    send_ref[...] = paired[:, pl.ds(other, SLOTS), :].astype(jnp.bfloat16)


def window_scratch(own, cols):
    frames, rows, _, channels = own.shape
    return pltpu.VMEM((frames + 2, rows + 2, cols, 3 * channels), jnp.bfloat16)


def input_grad(own, before, after, kernel, pre, width, begin):
    frames, rows, _, channels = own.shape
    cols = before.shape[1]
    flops = 2 * TAPS * frames * rows * cols * channels * channels
    taps = kernel.reshape(TAPS, channels, channels)
    if pre is None:
        shape = jax.ShapeDtypeStruct((frames, rows, width, channels), jnp.bfloat16)
        outs, operands = (shape,), (own, before, after, taps)
    else:
        shape = jax.ShapeDtypeStruct((frames, rows, cols, channels), jnp.bfloat16)
        edge = jax.ShapeDtypeStruct((frames, cols, channels), jnp.bfloat16)
        outs, operands = (shape, edge, edge), (own, before, after, taps, pre)
    body = functools.partial(input_grad_kernel, begin=begin)
    scratch = [window_scratch(own, cols)]
    return call(body, outs, operands, flops, scratch)


def kernel_grad(half, own, before, after, saved, activate, width, begin):
    frames, rows, _, channels = own.shape
    cols = before.shape[1]
    flops = 2 * TAPS * frames * rows * width * channels * channels
    shape = (channels // 2, SLOTS, channels)
    outs = (jax.ShapeDtypeStruct(shape, jnp.float32), jax.ShapeDtypeStruct(shape, jnp.bfloat16))
    body = functools.partial(kernel_grad_kernel, activate=activate, width=width, begin=begin)
    scratch = [
        window_scratch(own, cols),
        pltpu.VMEM((channels * SLOTS, channels), jnp.float32),
    ]
    return call(body, outs, (own, before, after, saved), flops, scratch, scalar=half)


def swapped(x, bit):
    return lax.ppermute(x, "ta", [(i, i ^ bit) for i in range(lax.axis_size("ta"))])


def row_halo(first, final):
    peers = lax.axis_size("ha")
    before = lax.ppermute(final, "ha", [(i, i + 1) for i in range(peers - 1)])
    after = lax.ppermute(first, "ha", [(i + 1, i) for i in range(peers - 1)])
    return before, after


def across(x):
    return lax.all_to_all(x, "ta", 0, 0, tiled=True)


def returned(blocks):
    parts = blocks.shape[0]
    me = lax.axis_index("ta")
    pieces = [lax.dynamic_index_in_dim(blocks, me, 0, False)]
    for bits in range(1, parts):
        pieces.append(swapped(lax.dynamic_index_in_dim(blocks, me ^ bits, 0, False), bits))
    stacked = jnp.stack(pieces)
    ordered = [lax.dynamic_index_in_dim(stacked, me ^ part, 0, False) for part in range(parts)]
    return jnp.concatenate(ordered, 2)


def fold_rows(joined, upper):
    peers = lax.axis_size("ha")
    size = peers // 2
    send = lax.dynamic_slice_in_dim(joined, (1 - upper) * size, size, 0)
    keep = lax.dynamic_slice_in_dim(joined, upper * size, size, 0)
    other = lax.ppermute(send, "ha", [(i, (i + size) % peers) for i in range(peers)])
    total = keep.astype(jnp.float32) + other.astype(jnp.float32)
    return total.astype(jnp.bfloat16)


def shards(
    layer_input, pre_one, pre_two, pre_three, kernel_one, kernel_two, kernel_three, upstream
):
    frames, rows, columns, channels = layer_input.shape
    parts = lax.axis_size("ta")
    width = columns // parts
    cells_total = layer_input.size // channels * parts * lax.axis_size("ha")
    norm_scale = 1.0 / math.sqrt(cells_total)
    half = (lax.axis_index("ta") % 2).astype(jnp.int32)
    upper = (lax.axis_index("ha") // (lax.axis_size("ha") // 2)).astype(jnp.int32)
    wide = width + 2 * HALO
    first_shape = jax.ShapeDtypeStruct((parts, frames, rows, 2 * wide, channels), jnp.bfloat16)
    second_shape = (parts, frames, rows, wide + width, channels)
    second_shape = jax.ShapeDtypeStruct(second_shape, jnp.bfloat16)

    def gathered(block):
        moved = across(block)
        return moved.reshape((parts * frames,) + moved.shape[2:])

    block = call(split_first, (first_shape,), (upstream, pre_three, pre_two), 10**6)[0]
    grad = gathered(block)
    block = call(split_second, (second_shape,), (pre_one, layer_input), 10**6)[0]
    before, after = row_halo(grad[:, 0, 0:wide], grad[:, rows - 1, 0:wide])
    second = gathered(block)

    def kernel_term(saved, activate, begin):
        keep, send = kernel_grad(
            half.reshape(1), grad, before, after, saved, activate, width, begin
        )
        return keep + swapped(send, 1).astype(jnp.float32)

    saved = grad
    outs = input_grad(grad, before, after, kernel_three, saved, width, wide)
    term_three = kernel_term(saved, True, wide).astype(jnp.bfloat16)
    term_three = fold_rows(term_three, upper)
    grad = outs[0]
    before, after = row_halo(outs[1], outs[2])
    outs = input_grad(grad, before, after, kernel_two, second, width, 0)
    term_two = kernel_term(second, True, 0).astype(jnp.bfloat16)
    term_two = fold_rows(term_two, upper)
    grad = outs[0]
    before, after = row_halo(outs[1], outs[2])
    late = kernel_term(second, False, wide).astype(jnp.bfloat16)
    late = fold_rows(late, upper)
    size = lax.axis_size("ha") // 2
    halves = [[start + i for i in range(size)] for start in (0, size)]
    terms = lax.all_to_all(
        jnp.concatenate([term_three, term_two, late], 1), "ha", 0, 0, axis_index_groups=halves, tiled=True
    )
    own = input_grad(grad, before, after, kernel_one, None, width, 0)[0]
    back = returned(own.reshape((parts, frames) + own.shape[1:]))
    back = back.reshape(layer_input.shape)
    mine = jnp.sum(terms.astype(jnp.float32), 0).reshape(3, SLOTS, channels)
    mine = mine + swapped(mine, 2)
    theirs = swapped(mine, 1)
    low = jnp.where(half == 0, mine, theirs)
    high = jnp.where(half == 0, theirs, mine)
    both = jnp.stack([low, high], 2)[:, :TAPS] * norm_scale
    grads = [both[layer].reshape(3, 3, 3, 2, channels) for layer in range(3)]
    return (back, grads[2], grads[1], grads[0])


def solution(mesh):
    cells = P("ta", "ha", None, None)
    grads = P(None, None, None, "ha", None)
    return jax.shard_map(
        shards,
        mesh=mesh,
        in_specs=(cells, cells, cells, cells, P(), P(), P(), cells),
        out_specs=(cells, grads, grads, grads),
        check_vma=False,
    )
```

time: 406 us -> 152 us (0.37)
  the two profiles are of different devices: /device:TPU:97 before, /device:TPU:1 now
where the time goes in v1:
time: 152 us; the launch traced here: 151 us
  starting transfers between devices  59.6 us (39%)
  waiting for transfers between devices  51.1 us (34%)
  Pallas kernels  24 us (16%)
  local copies, waits for them, and re-layouts  11 us (7%)
  other arithmetic  4.75 us (3%)
    pallas_call x8, Pallas kernels, call(): pl.pallas_call(kernel, out_shape=tuple(out_shape), in_specs=[SMEM] * skip...  24 us
    ppermute x8, starting transfers between devices, swapped(): lax.ppermute(x, 'ta', [(i, i ^ bit) for i in range(lax.axis_size('ta'))])  14.3 us
    ppermute x3, starting transfers between devices, fold_rows(): lax.ppermute(send, 'ha', [(i, (i + size) % peers) for i in range(peers)])  14.2 us
    ppermute x3, waiting for transfers between devices, fold_rows(): lax.ppermute(send, 'ha', [(i, (i + size) % peers) for i in range(peers)])  14.2 us
    all_to_all x2, waiting for transfers between devices, across(): return lax.all_to_all(x, 'ta', 0, 0, tiled=True)  11.2 us
    all_to_all x2, starting transfers between devices, across(): return lax.all_to_all(x, 'ta', 0, 0, tiled=True)  11.2 us
    ppermute x3, starting transfers between devices, row_halo(): before = lax.ppermute(final, 'ha', [(i, i + 1) for i in range(peers - 1)])  10.8 us
    unnamed x46, local copies, waits for them, and re-layouts  10.3 us
  transfers between devices with their start and end apart: 20, of which 13 were waited for; matrix products, arithmetic and copies ran while one was open for 2% of the time, Pallas kernels for 15%

profile of v1, /device:TPU:1, one launch (start us, length us, event | category | flops | bytes accessed | tf_op | source)
XLA Modules:
  0.0 151.4 jit_solution(1044162876534870904)
XLA Ops:
  4.6 6.8 %all-to-all-start = ((bf16[4,2,3,128,128]{4,3,2,1,0:T(8,128)(2,1)}), bf16[4,2,3,128,128]{4,3,2,1,0:T(8,128)(2,1)S(1)}, u32[]{:S(2)}, u32[]{:S(2)}) async-start(bf16[4,2,3,128,128]{4,3,2,1,0:T(8,128)(2,1)} %shard_map.111), calls=%async_computation | async-start | bytes 1572864 | tf_op jit(solution)/shard_map/all_to_all | solution.py:223
  12.4 11.2 %all-to-all-done = bf16[4,2,3,128,128]{4,3,2,1,0:T(8,128)(2,1)S(1)} async-done(((bf16[4,2,3,128,128]{4,3,2,1,0:T(8,128)(2,1)}), bf16[4,2,3,128,128]{4,3,2,1,0:T(8,128)(2,1)S(1)}, u32[]{:S(2)}, u32[]{:S(2)}) %all-to-all-start) | async-done | bytes 786464 | tf_op jit(solution)/shard_map/all_to_all | solution.py:223
  23.6 4.4 %all-to-all-start.1 = ((bf16[4,2,3,112,128]{4,3,2,1,0:T(8,128)(2,1)}), bf16[4,2,3,112,128]{4,3,2,1,0:T(8,128)(2,1)S(1)}, u32[]{:S(2)}, u32[]{:S(2)}) async-start(bf16[4,2,3,112,128]{4,3,2,1,0:T(8,128)(2,1)} %shard_map.113), calls=%async_computation.1 | async-start | bytes 1376256 | tf_op jit(solution)/shard_map/all_to_all | solution.py:223
  28.0 2.4 %collective-permute-start = (bf16[8,64,128]{2,1,0:T(8,128)(2,1)S(1)}, bf16[8,64,128]{2,1,0:T(8,128)(2,1)S(1)}, u32[]{:S(2)}, u32[]{:S(2)}) collective-permute-start(bf16[8,64,128]{2,1,0:T(8,128)(2,1)S(1)} %get-tuple-element.29), channel_id=1, source_target_pairs={{0,4},{4,8},{8,12},{12,16},{16,20},{20,24},{24,28},{28,32},{32,36}... | collective-permute-start | bytes 393224 | tf_op jit(solution)/shard_map/ppermute | solution.py:217
  30.5 1.3 collective-permute-start.1
  31.8 1.5 collective-permute-done.refs_1_.refs_2_
  33.3 3.8 %collective-permute-done.1.refs_2_.refs_3_ = bf16[8,64,128]{2,1,0:T(8,128)(2,1)S(1)} collective-permute-done((bf16[8,64,128]{2,1,0:T(8,128)(2,1)S(1)}, bf16[8,64,128]{2,1,0:T(8,128)(2,1)S(1)}, u32[]{:S(2)}, u32[]{:S(2)}) %collective-permute-start.1) | collective-permute-done | bytes 131104 | tf_op jit(solution)/shard_map/ppermute | solution.py:218
  37.1 4.1 %shard_map.116 = (f32[64,32,128]{2,1,0:T(8,128)S(1)}, bf16[64,32,128]{2,1,0:T(8,128)(2,1)}) custom-call(s32[1]{0:T(128)} %bitcast.18.refs_0_, bf16[8,3,128,128]{3,2,1,0:T(8,128)(2,1)S(1)} %bitcast.37, bf16[8,64,128]{2,1,0:T(8,128)(2,1)S(1)} %collective-permute-done.refs_1_.refs_2_, bf16[8,64,128]{2,1,0:T(8,128)(2,1)S(1)} %collective-permute-done.1.refs_2_.refs_3_, ...), custom_call_target="tpu_custom_call" | custom-call | flops 1019215872 | bytes 3407872 | tf_op jit(solution)/shard_map/pallas_call | solution.py:34
  43.3 3.7 %shard_map.112 = (bf16[8,3,64,128]{3,2,1,0:T(8,128)(2,1)S(1)}, bf16[8,64,128]{2,1,0:T(8,128)(2,1)}, bf16[8,64,128]{2,1,0:T(8,128)(2,1)}) custom-call(bf16[8,3,128,128]{3,2,1,0:T(8,128)(2,1)S(1)} %bitcast.39, bf16[8,64,128]{2,1,0:T(8,128)(2,1)S(1)} %collective-permute-done.refs_1_.refs_2_, bf16[8,64,128]{2,1,0:T(8,128)(2,1)S(1)} %copy-done.12, ...), custom_call_target="tpu_custom_call" | custom-call | flops 1358954496 | bytes 3375104 | tf_op jit(solution)/shard_map/pallas_call | solution.py:34
  47.8 3.1 %collective-permute-start.2 = (bf16[8,64,128]{2,1,0:T(8,128)(2,1)}, bf16[8,64,128]{2,1,0:T(8,128)(2,1)S(1)}, u32[]{:S(2)}, u32[]{:S(2)}) collective-permute-start(bf16[8,64,128]{2,1,0:T(8,128)(2,1)} %get-tuple-element.17), channel_id=1, source_target_pairs={{0,4},{4,8},{8,12},{12,16},{16,20},{20,24},{24,28},{28,32},{32,36}... | collective-permute-start | bytes 393224 | tf_op jit(solution)/shard_map/ppermute | solution.py:217
  50.9 1.3 collective-permute-start.3
  52.2 1.8 %collective-permute-done.2.refs_1_.refs_2_ = bf16[8,64,128]{2,1,0:T(8,128)(2,1)S(1)} collective-permute-done((bf16[8,64,128]{2,1,0:T(8,128)(2,1)}, bf16[8,64,128]{2,1,0:T(8,128)(2,1)S(1)}, u32[]{:S(2)}, u32[]{:S(2)}) %collective-permute-start.2) | collective-permute-done | bytes 131104 | tf_op jit(solution)/shard_map/ppermute | solution.py:217
  54.0 3.7 %collective-permute-done.3.refs_2_.refs_3_ = bf16[8,64,128]{2,1,0:T(8,128)(2,1)S(1)} collective-permute-done((bf16[8,64,128]{2,1,0:T(8,128)(2,1)}, bf16[8,64,128]{2,1,0:T(8,128)(2,1)S(1)}, u32[]{:S(2)}, u32[]{:S(2)}) %collective-permute-start.3) | collective-permute-done | bytes 131104 | tf_op jit(solution)/shard_map/ppermute | solution.py:218
  58.8 3.7 %shard_map.114 = (bf16[8,3,64,128]{3,2,1,0:T(8,128)(2,1)S(1)}, bf16[8,64,128]{2,1,0:T(8,128)(2,1)}, bf16[8,64,128]{2,1,0:T(8,128)(2,1)}) custom-call(bf16[8,3,64,128]{3,2,1,0:T(8,128)(2,1)S(1)} %copy-done.18, bf16[8,64,128]{2,1,0:T(8,128)(2,1)S(1)} %collective-permute-done.2.refs_1_.refs_2_, bf16[8,64,128]{2,1,0:T(8,128)(2,1)S(1)} %collective-permute-done.3.refs_2_.refs_3_, ...), custom_call_target="tpu_custom_call" | custom-call | flops 1358954496 | bytes 2883584 | tf_op jit(solution)/shard_map/pallas_call | solution.py:34
  63.2 5.3 %collective-permute-start.4 = (bf16[8,64,128]{2,1,0:T(8,128)(2,1)}, bf16[8,64,128]{2,1,0:T(8,128)(2,1)S(1)}, u32[]{:S(2)}, u32[]{:S(2)}) collective-permute-start(bf16[8,64,128]{2,1,0:T(8,128)(2,1)} %get-tuple-element.20), channel_id=1, source_target_pairs={{0,4},{4,8},{8,12},{12,16},{16,20},{20,24},{24,28},{28,32},{32,36}... | collective-permute-start | bytes 393224 | tf_op jit(solution)/shard_map/ppermute | solution.py:217
  68.5 1.5 collective-permute-start.5
  73.0 3.2 %shard_map.117 = (f32[64,32,128]{2,1,0:T(8,128)S(1)}, bf16[64,32,128]{2,1,0:T(8,128)(2,1)S(1)}) custom-call(s32[1]{0:T(128)} %bitcast.18.refs_0_, bf16[8,3,64,128]{3,2,1,0:T(8,128)(2,1)S(1)} %copy-done.19, bf16[8,64,128]{2,1,0:T(8,128)(2,1)S(1)} %copy-done.14, bf16[8,64,128]{2,1,0:T(8,128)(2,1)S(1)} %copy-done.16, bf16[8,3,112,128]{3,2,1,0:T(8,128)(2,1)S(1)} %bitcast.42), custom_call_target="tpu_custom_call" | custom-call | flops 1019215872 | bytes 2916352 | tf_op jit(solution)/shard_map/pallas_call | solution.py:34
  78.4 4.0 %shard_map.118 = (f32[64,32,128]{2,1,0:T(8,128)S(1)}, bf16[64,32,128]{2,1,0:T(8,128)(2,1)S(1)}) custom-call(s32[1]{0:T(128)} %bitcast.18.refs_0_, bf16[8,3,64,128]{3,2,1,0:T(8,128)(2,1)S(1)} %copy-done.21, bf16[8,64,128]{2,1,0:T(8,128)(2,1)S(1)} %collective-permute-done.4.refs_1_.refs_2_, bf16[8,64,128]{2,1,0:T(8,128)(2,1)} %collective-permute-done.5.refs_2_.refs_3_, ...), custom_call_target="tpu_custom_call" | custom-call | flops 1019215872 | bytes 2916352 | tf_op jit(solution)/shard_map/pallas_call | solution.py:34
  83.9 12.6 %collective-permute-start.10 = (bf16[32,32,128]{2,1,0:T(8,128)(2,1)S(1)}, bf16[32,32,128]{2,1,0:T(8,128)(2,1)S(1)}, u32[]{:S(2)}, u32[]{:S(2)}) collective-permute-start(bf16[32,32,128]{2,1,0:T(8,128)(2,1)S(1)} %constant_dynamic-slice_fusion.2), channel_id=1, source_target_pairs={{0,128},{4,132},{8,136},{12,140},{16,144},{20,148},{24,152},{28,15... | collective-permute-start | bytes 786440 | tf_op jit(solution)/shard_map/ppermute | solution.py:242
  98.0 1.5 %collective-permute-start.14 = (bf16[32,32,128]{2,1,0:T(8,128)(2,1)S(1)}, bf16[32,32,128]{2,1,0:T(8,128)(2,1)S(1)}, u32[]{:S(2)}, u32[]{:S(2)}) collective-permute-start(bf16[32,32,128]{2,1,0:T(8,128)(2,1)S(1)} %constant_dynamic-slice_fusion), channel_id=1, source_target_pairs={{0,128},{4,132},{8,136},{12,140},{16,144},{20,148},{24,152},{28,15... | collective-permute-start | bytes 786440 | tf_op jit(solution)/shard_map/ppermute | solution.py:242
  99.6 3.1 %collective-permute-done.10 = bf16[32,32,128]{2,1,0:T(8,128)(2,1)S(1)} collective-permute-done((bf16[32,32,128]{2,1,0:T(8,128)(2,1)S(1)}, bf16[32,32,128]{2,1,0:T(8,128)(2,1)S(1)}, u32[]{:S(2)}, u32[]{:S(2)}) %collective-permute-start.10) | collective-permute-done | bytes 262176 | tf_op jit(solution)/shard_map/ppermute | solution.py:242
  102.8 5.5 %collective-permute-done.12 = bf16[32,32,128]{2,1,0:T(8,128)(2,1)S(1)} collective-permute-done((bf16[32,32,128]{2,1,0:T(8,128)(2,1)S(1)}, bf16[32,32,128]{2,1,0:T(8,128)(2,1)S(1)}, u32[]{:S(2)}, u32[]{:S(2)}) %collective-permute-start.12) | collective-permute-done | bytes 262176 | tf_op jit(solution)/shard_map/ppermute | solution.py:242
  108.4 5.5 %collective-permute-done.14 = bf16[32,32,128]{2,1,0:T(8,128)(2,1)S(1)} collective-permute-done((bf16[32,32,128]{2,1,0:T(8,128)(2,1)S(1)}, bf16[32,32,128]{2,1,0:T(8,128)(2,1)S(1)}, u32[]{:S(2)}, u32[]{:S(2)}) %collective-permute-start.14) | collective-permute-done | bytes 262176 | tf_op jit(solution)/shard_map/ppermute | solution.py:242
  115.0 5.0 %all-to-all-start.2 = ((bf16[32,96,128]{2,1,0:T(8,128)(2,1)}), bf16[32,96,128]{2,1,0:T(8,128)(2,1)S(1)}, u32[]{:S(2)}, u32[]{:S(2)}) async-start(bf16[32,96,128]{2,1,0:T(8,128)(2,1)} %pad_maximum_fusion), calls=%async_computation.2 | async-start | bytes 1572864 | tf_op jit(solution)/shard_map/all_to_all | solution.py:293
  120.0 3.2 %shard_map.115 = bf16[8,3,48,128]{3,2,1,0:T(8,128)(2,1)S(1)} custom-call(bf16[8,3,64,128]{3,2,1,0:T(8,128)(2,1)S(1)} %copy-done.22, bf16[8,64,128]{2,1,0:T(8,128)(2,1)S(1)} %collective-permute-done.4.refs_1_.refs_2_, bf16[8,64,128]{2,1,0:T(8,128)(2,1)} %collective-permute-done.5.refs_2_.refs_3_, bf16[27,128,128]{2,1,0:T(8,128)(2,1)S(1)} %bitcast.47), custom_call_target="tpu_custom_call" | custom-call | flops 1358954496 | bytes 1835008 | tf_op jit(solution)/shard_map/pallas_call | solution.py:34
  123.2 3.2 %collective-permute-start.7 = (bf16[2,3,48,128]{3,2,1,0:T(8,128)(2,1)S(1)}, bf16[2,3,48,128]{3,2,1,0:T(8,128)(2,1)S(1)}, u32[]{:S(2)}, u32[]{:S(2)}) collective-permute-start(bf16[2,3,48,128]{3,2,1,0:T(8,128)(2,1)S(1)} %get-tuple-element.36), channel_id=1, source_target_pairs={{0,2},{1,3},{2,0},{3,1},{4,6},{5,7},{6,4},{7,5},{8,10},{9,11},{10,... | collective-permute-start | bytes 221192 | tf_op jit(solution)/shard_map/ppermute | solution.py:212
  126.4 1.4 collective-permute-start.8
  128.5 3.5 %collective-permute-done.8 = bf16[2,3,48,128]{3,2,1,0:T(8,128)(2,1)S(1)} collective-permute-done((bf16[2,3,48,128]{3,2,1,0:T(8,128)(2,1)S(1)}, bf16[2,3,48,128]{3,2,1,0:T(8,128)(2,1)S(1)}, u32[]{:S(2)}, u32[]{:S(2)}) %collective-permute-start.8) | collective-permute-done | bytes 73760 | tf_op jit(solution)/shard_map/ppermute | solution.py:212
  132.1 8.9 %all-to-all-done.2 = bf16[32,96,128]{2,1,0:T(8,128)(2,1)S(1)} async-done(((bf16[32,96,128]{2,1,0:T(8,128)(2,1)}), bf16[32,96,128]{2,1,0:T(8,128)(2,1)S(1)}, u32[]{:S(2)}, u32[]{:S(2)}) %all-to-all-start.2) | async-done | bytes 786464 | tf_op jit(solution)/shard_map/all_to_all | solution.py:293
  141.1 3.0 %collective-permute-start.15 = (f32[3,32,128]{2,1,0:T(8,128)S(1)}, f32[3,32,128]{2,1,0:T(8,128)S(1)}, u32[]{:S(2)}, u32[]{:S(2)}) collective-permute-start(f32[3,32,128]{2,1,0:T(8,128)S(1)} %bitcast.48), channel_id=1, source_target_pairs={{0,2},{1,3},{2,0},{3,1},{4,6},{5,7},{6,4},{7,5},{8,10},{9,11},{10,... | collective-permute-start | bytes 147464 | tf_op jit(solution)/shard_map/ppermute | solution.py:212
  144.1 1.5 %collective-permute-done.15 = f32[3,32,128]{2,1,0:T(8,128)S(1)} collective-permute-done((f32[3,32,128]{2,1,0:T(8,128)S(1)}, f32[3,32,128]{2,1,0:T(8,128)S(1)}, u32[]{:S(2)}, u32[]{:S(2)}) %collective-permute-start.15) | collective-permute-done | bytes 49184 | tf_op jit(solution)/shard_map/ppermute | solution.py:212
  145.7 4.1 %collective-permute-start.16 = (f32[3,32,128]{2,1,0:T(8,128)S(1)}, f32[3,32,128]{2,1,0:T(8,128)S(1)}, u32[]{:S(2)}, u32[]{:S(2)}) collective-permute-start(f32[3,32,128]{2,1,0:T(8,128)S(1)} %add.66), channel_id=1, source_target_pairs={{0,1},{1,0},{2,3},{3,2},{4,5},{5,4},{6,7},{7,6},{8,9},{9,8},{10,11... | collective-permute-start | bytes 147464 | tf_op jit(solution)/shard_map/ppermute | solution.py:212
  (82 shorter events, 21.4 us)
Async XLA Ops:
  4.6 6.8 %copy-start.6 = (bf16[2,3,192,128]{3,2,1,0:T(8,128)(2,1)S(1)}, bf16[2,3,192,128]{3,2,1,0:T(8,128)(2,1)}, u32[]{:S(2)}) copy-start(bf16[2,3,192,128]{3,2,1,0:T(8,128)(2,1)} %refs_0_.3) | copy-start | bytes 884740
  4.6 6.8 %copy-start.7 = (bf16[2,3,192,128]{3,2,1,0:T(8,128)(2,1)S(1)}, bf16[2,3,192,128]{3,2,1,0:T(8,128)(2,1)}, u32[]{:S(2)}) copy-start(bf16[2,3,192,128]{3,2,1,0:T(8,128)(2,1)} %refs_1_.3) | copy-start | bytes 884740
  4.6 19.0 %all-to-all-start = ((bf16[4,2,3,128,128]{4,3,2,1,0:T(8,128)(2,1)}), bf16[4,2,3,128,128]{4,3,2,1,0:T(8,128)(2,1)S(1)}, u32[]{:S(2)}, u32[]{:S(2)}) async-start(bf16[4,2,3,128,128]{4,3,2,1,0:T(8,128)(2,1)} %shard_map.111), calls=%async_computation | async-start | bytes 1572864 | tf_op jit(solution)/shard_map/all_to_all | solution.py:223
  23.6 28.6 %all-to-all-start.1 = ((bf16[4,2,3,112,128]{4,3,2,1,0:T(8,128)(2,1)}), bf16[4,2,3,112,128]{4,3,2,1,0:T(8,128)(2,1)S(1)}, u32[]{:S(2)}, u32[]{:S(2)}) async-start(bf16[4,2,3,112,128]{4,3,2,1,0:T(8,128)(2,1)} %shard_map.113), calls=%async_computation.1 | async-start | bytes 1376256 | tf_op jit(solution)/shard_map/all_to_all | solution.py:223
  28.0 5.2 %collective-permute-start = (bf16[8,64,128]{2,1,0:T(8,128)(2,1)S(1)}, bf16[8,64,128]{2,1,0:T(8,128)(2,1)S(1)}, u32[]{:S(2)}, u32[]{:S(2)}) collective-permute-start(bf16[8,64,128]{2,1,0:T(8,128)(2,1)S(1)} %get-tuple-element.29), channel_id=1, source_target_pairs={{0,4},{4,8},{8,12},{12,16},{16,20},{20,24},{24,28},{28,32},{32,36}... | collective-permute-start | bytes 393224 | tf_op jit(solution)/shard_map/ppermute | solution.py:217
  30.5 6.6 %collective-permute-start.1 = (bf16[8,64,128]{2,1,0:T(8,128)(2,1)S(1)}, bf16[8,64,128]{2,1,0:T(8,128)(2,1)S(1)}, u32[]{:S(2)}, u32[]{:S(2)}) collective-permute-start(bf16[8,64,128]{2,1,0:T(8,128)(2,1)S(1)} %get-tuple-element.28), channel_id=1, source_target_pairs={{4,0},{8,4},{12,8},{16,12},{20,16},{24,20},{28,24},{32,28},{36,32}... | collective-permute-start | bytes 393224 | tf_op jit(solution)/shard_map/ppermute | solution.py:218
  37.1 4.1 %copy-start.11 = (bf16[8,64,128]{2,1,0:T(8,128)(2,1)}, bf16[8,64,128]{2,1,0:T(8,128)(2,1)S(1)}, u32[]{:S(2)}) copy-start(bf16[8,64,128]{2,1,0:T(8,128)(2,1)S(1)} %collective-permute-done.1.refs_2_.refs_3_) | copy-start | bytes 393220
  37.1 5.3 %copy-start.8 = (bf16[3,3,3,128,128]{4,3,2,1,0:T(8,128)(2,1)S(1)}, bf16[3,3,3,128,128]{4,3,2,1,0:T(8,128)(2,1)}, u32[]{:S(2)}) copy-start(bf16[3,3,3,128,128]{4,3,2,1,0:T(8,128)(2,1)} %param.14) | copy-start | bytes 2654212
  41.2 41.5 %collective-permute-start.9 = (bf16[64,32,128]{2,1,0:T(8,128)(2,1)}, bf16[64,32,128]{2,1,0:T(8,128)(2,1)}, u32[]{:S(2)}, u32[]{:S(2)}) collective-permute-start(bf16[64,32,128]{2,1,0:T(8,128)(2,1)} %get-tuple-element.23), channel_id=1, source_target_pairs={{0,1},{1,0},{2,3},{3,2},{4,5},{5,4},{6,7},{7,6},{8,9},{9,8},{10,11... | collective-permute-start | bytes 1572872 | tf_op jit(solution)/shard_map/ppermute | solution.py:212
  43.3 14.5 %copy-start.9 = (bf16[3,3,3,128,128]{4,3,2,1,0:T(8,128)(2,1)S(1)}, bf16[3,3,3,128,128]{4,3,2,1,0:T(8,128)(2,1)}, u32[]{:S(2)}) copy-start(bf16[3,3,3,128,128]{4,3,2,1,0:T(8,128)(2,1)} %param.13) | copy-start | bytes 2654212
  47.8 6.3 %collective-permute-start.2 = (bf16[8,64,128]{2,1,0:T(8,128)(2,1)}, bf16[8,64,128]{2,1,0:T(8,128)(2,1)S(1)}, u32[]{:S(2)}, u32[]{:S(2)}) collective-permute-start(bf16[8,64,128]{2,1,0:T(8,128)(2,1)} %get-tuple-element.17), channel_id=1, source_target_pairs={{0,4},{4,8},{8,12},{12,16},{16,20},{20,24},{24,28},{28,32},{32,36}... | collective-permute-start | bytes 393224 | tf_op jit(solution)/shard_map/ppermute | solution.py:217
  50.9 6.9 %collective-permute-start.3 = (bf16[8,64,128]{2,1,0:T(8,128)(2,1)}, bf16[8,64,128]{2,1,0:T(8,128)(2,1)S(1)}, u32[]{:S(2)}, u32[]{:S(2)}) collective-permute-start(bf16[8,64,128]{2,1,0:T(8,128)(2,1)} %get-tuple-element.18), channel_id=1, source_target_pairs={{4,0},{8,4},{12,8},{16,12},{20,16},{24,20},{28,24},{32,28},{36,32}... | collective-permute-start | bytes 393224 | tf_op jit(solution)/shard_map/ppermute | solution.py:218
  52.2 10.3 %copy-start = (bf16[4,2,3,112,128]{4,3,2,1,0:T(8,128)(2,1)}, bf16[4,2,3,112,128]{4,3,2,1,0:T(8,128)(2,1)S(1)}, u32[]{:S(2)}) copy-start(bf16[4,2,3,112,128]{4,3,2,1,0:T(8,128)(2,1)S(1)} %all-to-all-done.1) | copy-start | bytes 2064388
  54.0 8.5 %copy-start.13 = (bf16[8,64,128]{2,1,0:T(8,128)(2,1)}, bf16[8,64,128]{2,1,0:T(8,128)(2,1)S(1)}, u32[]{:S(2)}) copy-start(bf16[8,64,128]{2,1,0:T(8,128)(2,1)S(1)} %collective-permute-done.2.refs_1_.refs_2_) | copy-start | bytes 393220
  57.7 4.7 %copy-start.15 = (bf16[8,64,128]{2,1,0:T(8,128)(2,1)}, bf16[8,64,128]{2,1,0:T(8,128)(2,1)S(1)}, u32[]{:S(2)}) copy-start(bf16[8,64,128]{2,1,0:T(8,128)(2,1)S(1)} %collective-permute-done.3.refs_2_.refs_3_) | copy-start | bytes 393220
  58.8 11.2 %copy-start.19 = (bf16[8,3,64,128]{3,2,1,0:T(8,128)(2,1)S(1)}, bf16[8,3,64,128]{3,2,1,0:T(8,128)(2,1)}, u32[]{:S(2)}) copy-start(bf16[8,3,64,128]{3,2,1,0:T(8,128)(2,1)} %copy-done.17) | copy-start | bytes 1179652
  63.2 14.2 %collective-permute-start.4 = (bf16[8,64,128]{2,1,0:T(8,128)(2,1)}, bf16[8,64,128]{2,1,0:T(8,128)(2,1)S(1)}, u32[]{:S(2)}, u32[]{:S(2)}) collective-permute-start(bf16[8,64,128]{2,1,0:T(8,128)(2,1)} %get-tuple-element.20), channel_id=1, source_target_pairs={{0,4},{4,8},{8,12},{12,16},{16,20},{20,24},{24,28},{28,32},{32,36}... | collective-permute-start | bytes 393224 | tf_op jit(solution)/shard_map/ppermute | solution.py:217
  68.5 8.9 %collective-permute-start.5 = (bf16[8,64,128]{2,1,0:T(8,128)(2,1)}, bf16[8,64,128]{2,1,0:T(8,128)(2,1)}, u32[]{:S(2)}, u32[]{:S(2)}) collective-permute-start(bf16[8,64,128]{2,1,0:T(8,128)(2,1)} %get-tuple-element.21), channel_id=1, source_target_pairs={{4,0},{8,4},{12,8},{16,12},{20,16},{24,20},{28,24},{32,28},{36,32}... | collective-permute-start | bytes 393224 | tf_op jit(solution)/shard_map/ppermute | solution.py:218
  72.9 4.5 %copy-start.2 = (bf16[4,2,3,112,128]{4,3,2,1,0:T(8,128)(2,1)S(1)}, bf16[4,2,3,112,128]{4,3,2,1,0:T(8,128)(2,1)}, u32[]{:S(2)}) copy-start(bf16[4,2,3,112,128]{4,3,2,1,0:T(8,128)(2,1)} %copy-done) | copy-start | bytes 2064388
  76.2 20.3 %collective-permute-start.11 = (bf16[64,32,128]{2,1,0:T(8,128)(2,1)S(1)}, bf16[64,32,128]{2,1,0:T(8,128)(2,1)}, u32[]{:S(2)}, u32[]{:S(2)}) collective-permute-start(bf16[64,32,128]{2,1,0:T(8,128)(2,1)S(1)} %get-tuple-element.25), channel_id=1, source_target_pairs={{0,1},{1,0},{2,3},{3,2},{4,5},{5,4},{6,7},{7,6},{8,9},{9,8},{10,11... | collective-permute-start | bytes 1572872 | tf_op jit(solution)/shard_map/ppermute | solution.py:212
  82.5 15.3 %collective-permute-start.13 = (bf16[64,32,128]{2,1,0:T(8,128)(2,1)S(1)}, bf16[64,32,128]{2,1,0:T(8,128)(2,1)S(1)}, u32[]{:S(2)}, u32[]{:S(2)}) collective-permute-start(bf16[64,32,128]{2,1,0:T(8,128)(2,1)S(1)} %get-tuple-element.27), channel_id=1, source_target_pairs={{0,1},{1,0},{2,3},{3,2},{4,5},{5,4},{6,7},{7,6},{8,9},{9,8},{10,11... | collective-permute-start | bytes 1572872 | tf_op jit(solution)/shard_map/ppermute | solution.py:212
  83.9 18.8 %collective-permute-start.10 = (bf16[32,32,128]{2,1,0:T(8,128)(2,1)S(1)}, bf16[32,32,128]{2,1,0:T(8,128)(2,1)S(1)}, u32[]{:S(2)}, u32[]{:S(2)}) collective-permute-start(bf16[32,32,128]{2,1,0:T(8,128)(2,1)S(1)} %constant_dynamic-slice_fusion.2), channel_id=1, source_target_pairs={{0,128},{4,132},{8,136},{12,140},{16,144},{20,148},{24,152},{28,15... | collective-permute-start | bytes 786440 | tf_op jit(solution)/shard_map/ppermute | solution.py:242
  97.7 10.6 %collective-permute-start.12 = (bf16[32,32,128]{2,1,0:T(8,128)(2,1)S(1)}, bf16[32,32,128]{2,1,0:T(8,128)(2,1)S(1)}, u32[]{:S(2)}, u32[]{:S(2)}) collective-permute-start(bf16[32,32,128]{2,1,0:T(8,128)(2,1)S(1)} %constant_dynamic-slice_fusion.1), channel_id=1, source_target_pairs={{0,128},{4,132},{8,136},{12,140},{16,144},{20,148},{24,152},{28,15... | collective-permute-start | bytes 786440 | tf_op jit(solution)/shard_map/ppermute | solution.py:242
  98.0 15.9 %collective-permute-start.14 = (bf16[32,32,128]{2,1,0:T(8,128)(2,1)S(1)}, bf16[32,32,128]{2,1,0:T(8,128)(2,1)S(1)}, u32[]{:S(2)}, u32[]{:S(2)}) collective-permute-start(bf16[32,32,128]{2,1,0:T(8,128)(2,1)S(1)} %constant_dynamic-slice_fusion), channel_id=1, source_target_pairs={{0,128},{4,132},{8,136},{12,140},{16,144},{20,148},{24,152},{28,15... | collective-permute-start | bytes 786440 | tf_op jit(solution)/shard_map/ppermute | solution.py:242
  115.0 5.0 %copy-start.10 = (bf16[3,3,3,128,128]{4,3,2,1,0:T(8,128)(2,1)S(1)}, bf16[3,3,3,128,128]{4,3,2,1,0:T(8,128)(2,1)}, u32[]{:S(2)}) copy-start(bf16[3,3,3,128,128]{4,3,2,1,0:T(8,128)(2,1)} %param.12) | copy-start | bytes 2654212
  115.0 5.0 %copy-start.22 = (bf16[8,3,64,128]{3,2,1,0:T(8,128)(2,1)S(1)}, bf16[8,3,64,128]{3,2,1,0:T(8,128)(2,1)}, u32[]{:S(2)}) copy-start(bf16[8,3,64,128]{3,2,1,0:T(8,128)(2,1)} %copy-done.20) | copy-start | bytes 1179652
  115.0 26.1 %all-to-all-start.2 = ((bf16[32,96,128]{2,1,0:T(8,128)(2,1)}), bf16[32,96,128]{2,1,0:T(8,128)(2,1)S(1)}, u32[]{:S(2)}, u32[]{:S(2)}) async-start(bf16[32,96,128]{2,1,0:T(8,128)(2,1)} %pad_maximum_fusion), calls=%async_computation.2 | async-start | bytes 1572864 | tf_op jit(solution)/shard_map/all_to_all | solution.py:293
  123.2 5.3 %collective-permute-start.7 = (bf16[2,3,48,128]{3,2,1,0:T(8,128)(2,1)S(1)}, bf16[2,3,48,128]{3,2,1,0:T(8,128)(2,1)S(1)}, u32[]{:S(2)}, u32[]{:S(2)}) collective-permute-start(bf16[2,3,48,128]{3,2,1,0:T(8,128)(2,1)S(1)} %get-tuple-element.36), channel_id=1, source_target_pairs={{0,2},{1,3},{2,0},{3,1},{4,6},{5,7},{6,4},{7,5},{8,10},{9,11},{10,... | collective-permute-start | bytes 221192 | tf_op jit(solution)/shard_map/ppermute | solution.py:212
  126.4 5.6 %collective-permute-start.8 = (bf16[2,3,48,128]{3,2,1,0:T(8,128)(2,1)S(1)}, bf16[2,3,48,128]{3,2,1,0:T(8,128)(2,1)S(1)}, u32[]{:S(2)}, u32[]{:S(2)}) collective-permute-start(bf16[2,3,48,128]{3,2,1,0:T(8,128)(2,1)S(1)} %get-tuple-element.35), channel_id=1, source_target_pairs={{0,3},{1,2},{2,1},{3,0},{4,7},{5,6},{6,5},{7,4},{8,11},{9,10},{10,... | collective-permute-start | bytes 221192 | tf_op jit(solution)/shard_map/ppermute | solution.py:212
  127.8 4.2 %collective-permute-start.6 = (bf16[2,3,48,128]{3,2,1,0:T(8,128)(2,1)S(1)}, bf16[2,3,48,128]{3,2,1,0:T(8,128)(2,1)S(1)}, u32[]{:S(2)}, u32[]{:S(2)}) collective-permute-start(bf16[2,3,48,128]{3,2,1,0:T(8,128)(2,1)S(1)} %get-tuple-element.37), channel_id=1, source_target_pairs={{0,1},{1,0},{2,3},{3,2},{4,5},{5,4},{6,7},{7,6},{8,9},{9,8},{10,11... | collective-permute-start | bytes 221192 | tf_op jit(solution)/shard_map/ppermute | solution.py:212
  141.1 4.5 %collective-permute-start.15 = (f32[3,32,128]{2,1,0:T(8,128)S(1)}, f32[3,32,128]{2,1,0:T(8,128)S(1)}, u32[]{:S(2)}, u32[]{:S(2)}) collective-permute-start(f32[3,32,128]{2,1,0:T(8,128)S(1)} %bitcast.48), channel_id=1, source_target_pairs={{0,2},{1,3},{2,0},{3,1},{4,6},{5,7},{6,4},{7,5},{8,10},{9,11},{10,... | collective-permute-start | bytes 147464 | tf_op jit(solution)/shard_map/ppermute | solution.py:212
  145.7 5.0 %collective-permute-start.16 = (f32[3,32,128]{2,1,0:T(8,128)S(1)}, f32[3,32,128]{2,1,0:T(8,128)S(1)}, u32[]{:S(2)}, u32[]{:S(2)}) collective-permute-start(f32[3,32,128]{2,1,0:T(8,128)S(1)} %add.66), channel_id=1, source_target_pairs={{0,1},{1,0},{2,3},{3,2},{4,5},{5,4},{6,7},{7,6},{8,9},{9,8},{10,11... | collective-permute-start | bytes 147464 | tf_op jit(solution)/shard_map/ppermute | solution.py:212
  (11 other events, 10.3 us)

commit v2 on v1

--- a/solution.py
+++ b/solution.py
@@ -16,28 +16,44 @@
 MIB = 1024 * 1024
 LIMIT = 18
 VMEM = pl.BlockSpec(memory_space=pltpu.VMEM)
+HBM = pl.BlockSpec(memory_space=pltpu.HBM)
 SMEM = pl.BlockSpec(memory_space=pltpu.SMEM)
 GROUPS = ((0, 1), (2, 3), (4, 5), (6, 7), (8,))
 
 
-def call(body, out_shape, operands, flops, scratch=(), scalar=None):
+def call(body, out_shape, operands, flops, scratch=(), scalar=None, fetched=False):
     moved = sum(a.size * a.dtype.itemsize for a in operands)
     moved += sum(math.prod(s.shape) * s.dtype.itemsize for s in out_shape)
     count, results = len(operands), len(out_shape)
     skip = 0 if scalar is None else 1
+    local = []
+    if fetched:
+        local = [pltpu.VMEM(a.shape, a.dtype) for a in operands]
+        local.append(pltpu.SemaphoreType.DMA((count,)))
 
     def kernel(*refs):
         loaded = refs[skip : skip + count]
         rest = refs[skip + count :]
+        if fetched:
+            semaphores = rest[-1]
+            sources, loaded, rest = loaded, rest[-1 - count : -1], rest[: -1 - count]
+            copies = [
+                pltpu.make_async_copy(source, local, semaphores.at[i])
+                for i, (source, local) in enumerate(zip(sources, loaded))
+            ]
+            for copy in copies:
+                copy.start()
+            for copy in copies:
+                copy.wait()
         body(*refs[:skip], loaded, rest[:results], *rest[results:])
 
     return pl.pallas_call(
         kernel,
         out_shape=tuple(out_shape),
-        in_specs=[SMEM] * skip + [VMEM] * count,
+        in_specs=[SMEM] * skip + [HBM if fetched else VMEM] * count,
         out_specs=(VMEM,) * results,
-        scratch_shapes=list(scratch),
-        compiler_params=pltpu.CompilerParams(vmem_limit_bytes=LIMIT * MIB),
+        scratch_shapes=list(scratch) + local,
+        compiler_params=pltpu.CompilerParams(vmem_limit_bytes=(60 if fetched else LIMIT) * MIB),
         cost_estimate=pl.CostEstimate(flops=flops, bytes_accessed=moved, transcendentals=0),
     )(*([] if scalar is None else [scalar]), *operands)
 
@@ -77,15 +93,25 @@
     split_columns(two[...], out_ref.at[:, :, :, wide : 2 * wide], OUTSIDE)
 
 
-def split_second(loaded, outs):
-    (out_ref,) = outs
-    one_ref, input_ref = loaded[0], loaded[1]
-    parts = out_ref.shape[0]
+def split_second(place_ref, loaded, outs, block_ref):
+    one_ref, input_ref = loaded
+    parts = len(outs)
     own = input_ref.shape[2] // parts
     wide = own + 2 * HALO
-    split_columns(one_ref[...], out_ref.at[:, :, :, 0:wide], OUTSIDE)
+    split_columns(one_ref[...], block_ref.at[:, :, :, 0:wide], OUTSIDE)
     for part in range(parts):
-        out_ref[part, :, :, wide : wide + own] = input_ref[:, :, part * own : (part + 1) * own]
+        block_ref[part, :, :, wide : wide + own] = input_ref[:, :, part * own : (part + 1) * own]
+    for bits, out_ref in enumerate(outs):
+        out_ref[...] = block_ref[place_ref[2] ^ bits]
+
+
+def in_order(place_ref, pieces, whole_ref):
+    frames = pieces[0].shape[0]
+    if len(pieces) == 1:
+        return pieces[0]
+    for bits, piece in enumerate(pieces):
+        whole_ref[pl.ds((place_ref[2] ^ bits) * frames, frames)] = piece[...]
+    return whole_ref
 
 
 def fill_window(own, before, after, window_ref):
@@ -104,7 +130,7 @@
             window_ref[frame, r, :, 2 * channels : 3 * channels] = preceding
 
 
-def input_grad_kernel(loaded, outs, window_ref, *, begin):
+def input_grad_kernel(place_ref, loaded, outs, window_ref, *whole_ref, begin):
     own, before, after, kernel, *pre = loaded
     frames, rows, channels = own.shape[0], own.shape[1], own.shape[3]
     cols = before.shape[1]
@@ -112,7 +138,7 @@
     fill_window(own, before, after, window_ref)
     kernel_ref = kernel
     if pre:
-        pre_ref = pre[0]
+        pre_ref = in_order(place_ref, pre, *whole_ref) if whole_ref else pre[0]
         first_ref, final_ref = outs[1:]
     weights = []
     for group in GROUPS:
@@ -143,14 +169,17 @@
             final_ref[f : f + step] = result[:, rows - 1]
 
 
-def kernel_grad_kernel(half_ref, loaded, outs, window_ref, spread_ref, *, activate, width, begin):
-    own, before, after, kept = loaded
+def kernel_grad_kernel(
+    place_ref, loaded, outs, window_ref, spread_ref, *whole_ref, activate, width, begin
+):
+    own, before, after, *kept = loaded
     keep_ref, send_ref = outs
     frames, rows, channels = own.shape[0], own.shape[1], own.shape[3]
     cells = frames * rows * width
     half = channels // 2
     fill_window(own, before, after, window_ref)
-    saved = kept[:, :, begin : begin + width]
+    kept_ref = in_order(place_ref, kept, *whole_ref) if whole_ref else kept[0]
+    saved = kept_ref[:, :, begin : begin + width]
     if activate:
         saved = silu(saved)
     left = saved.reshape(cells, channels).T
@@ -166,10 +195,13 @@
                 :, c * channels : (c + 1) * channels
             ]
     paired = spread_ref.reshape(half, 2 * SLOTS, channels)
-    mine = pl.multiple_of(half_ref[0] * SLOTS, SLOTS)
-    other = pl.multiple_of((1 - half_ref[0]) * SLOTS, SLOTS)
-    keep_ref[...] = paired[:, pl.ds(mine, SLOTS), :]
-    send_ref[...] = paired[:, pl.ds(other, SLOTS), :].astype(jnp.bfloat16)
+    mine = pl.multiple_of(place_ref[0] * SLOTS, SLOTS)
+    other = pl.multiple_of((1 - place_ref[0]) * SLOTS, SLOTS)
+    size = half // 2
+    for place, begin_row in enumerate(((1 - place_ref[1]) * size, place_ref[1] * size)):
+        span = pl.ds(begin_row, size)
+        keep_ref[place] = paired[span, pl.ds(mine, SLOTS), :]
+        send_ref[place] = paired[span, pl.ds(other, SLOTS), :].astype(jnp.bfloat16)
 
 
 def window_scratch(own, cols):
@@ -177,7 +209,14 @@
     return pltpu.VMEM((frames + 2, rows + 2, cols, 3 * channels), jnp.bfloat16)
 
 
-def input_grad(own, before, after, kernel, pre, width, begin):
+def whole_scratch(pieces):
+    if len(pieces) == 1:
+        return []
+    shape = (len(pieces) * pieces[0].shape[0],) + pieces[0].shape[1:]
+    return [pltpu.VMEM(shape, pieces[0].dtype)]
+
+
+def input_grad(place, own, before, after, kernel, pre, width, begin):
     frames, rows, _, channels = own.shape
     cols = before.shape[1]
     flops = 2 * TAPS * frames * rows * cols * channels * channels
@@ -188,24 +227,25 @@
     else:
         shape = jax.ShapeDtypeStruct((frames, rows, cols, channels), jnp.bfloat16)
         edge = jax.ShapeDtypeStruct((frames, cols, channels), jnp.bfloat16)
-        outs, operands = (shape, edge, edge), (own, before, after, taps, pre)
+        outs, operands = (shape, edge, edge), (own, before, after, taps, *pre)
     body = functools.partial(input_grad_kernel, begin=begin)
-    scratch = [window_scratch(own, cols)]
-    return call(body, outs, operands, flops, scratch)
-
-
-def kernel_grad(half, own, before, after, saved, activate, width, begin):
+    scratch = [window_scratch(own, cols)] + (whole_scratch(pre) if pre else [])
+    return call(body, outs, operands, flops, scratch, place)
+
+
+def kernel_grad(place, own, before, after, saved, activate, width, begin):
     frames, rows, _, channels = own.shape
     cols = before.shape[1]
     flops = 2 * TAPS * frames * rows * width * channels * channels
-    shape = (channels // 2, SLOTS, channels)
+    shape = (2, channels // 4, SLOTS, channels)
     outs = (jax.ShapeDtypeStruct(shape, jnp.float32), jax.ShapeDtypeStruct(shape, jnp.bfloat16))
     body = functools.partial(kernel_grad_kernel, activate=activate, width=width, begin=begin)
     scratch = [
         window_scratch(own, cols),
         pltpu.VMEM((channels * SLOTS, channels), jnp.float32),
     ]
-    return call(body, outs, (own, before, after, saved), flops, scratch, scalar=half)
+    scratch += whole_scratch(saved)
+    return call(body, outs, (own, before, after, *saved), flops, scratch, place)
 
 
 def swapped(x, bit):
@@ -234,13 +274,12 @@
     return jnp.concatenate(ordered, 2)
 
 
-def fold_rows(joined, upper):
+def fold_rows(keep, received):
     peers = lax.axis_size("ha")
     size = peers // 2
-    send = lax.dynamic_slice_in_dim(joined, (1 - upper) * size, size, 0)
-    keep = lax.dynamic_slice_in_dim(joined, upper * size, size, 0)
+    send = (keep[0] + received[0].astype(jnp.float32)).astype(jnp.bfloat16)
     other = lax.ppermute(send, "ha", [(i, (i + size) % peers) for i in range(peers)])
-    total = keep.astype(jnp.float32) + other.astype(jnp.float32)
+    total = keep[1] + received[1].astype(jnp.float32) + other.astype(jnp.float32)
     return total.astype(jnp.bfloat16)
 
 
@@ -256,49 +295,53 @@
     upper = (lax.axis_index("ha") // (lax.axis_size("ha") // 2)).astype(jnp.int32)
     wide = width + 2 * HALO
     first_shape = jax.ShapeDtypeStruct((parts, frames, rows, 2 * wide, channels), jnp.bfloat16)
-    second_shape = (parts, frames, rows, wide + width, channels)
-    second_shape = jax.ShapeDtypeStruct(second_shape, jnp.bfloat16)
+    second_shape = (frames, rows, wide + width, channels)
+    second_shapes = (jax.ShapeDtypeStruct(second_shape, jnp.bfloat16),) * parts
+    block_scratch = pltpu.VMEM((parts,) + second_shape, jnp.bfloat16)
+    place = jnp.stack([half, upper, lax.axis_index("ta").astype(jnp.int32)])
 
     def gathered(block):
         moved = across(block)
         return moved.reshape((parts * frames,) + moved.shape[2:])
 
-    block = call(split_first, (first_shape,), (upstream, pre_three, pre_two), 10**6)[0]
+    operands = (upstream, pre_three, pre_two)
+    block = call(split_first, (first_shape,), operands, 10**6, fetched=True)[0]
     grad = gathered(block)
-    block = call(split_second, (second_shape,), (pre_one, layer_input), 10**6)[0]
+    operands = (pre_one, layer_input)
+    blocks = call(split_second, second_shapes, operands, 10**6, [block_scratch], place)
     before, after = row_halo(grad[:, 0, 0:wide], grad[:, rows - 1, 0:wide])
-    second = gathered(block)
+    second = [blocks[0]] + [swapped(blocks[bits], bits) for bits in range(1, parts)]
 
     def kernel_term(saved, activate, begin):
         keep, send = kernel_grad(
-            half.reshape(1), grad, before, after, saved, activate, width, begin
+            place, grad, before, after, saved, activate, width, begin
         )
-        return keep + swapped(send, 1).astype(jnp.float32)
-
-    saved = grad
-    outs = input_grad(grad, before, after, kernel_three, saved, width, wide)
-    term_three = kernel_term(saved, True, wide).astype(jnp.bfloat16)
-    term_three = fold_rows(term_three, upper)
+        return keep, swapped(send, 1)
+
+    saved = [grad]
+    outs = input_grad(place, grad, before, after, kernel_three, saved, width, wide)
+    term_three = kernel_term(saved, True, wide)
+    term_three = fold_rows(*term_three)
     grad = outs[0]
     before, after = row_halo(outs[1], outs[2])
-    outs = input_grad(grad, before, after, kernel_two, second, width, 0)
-    term_two = kernel_term(second, True, 0).astype(jnp.bfloat16)
-    term_two = fold_rows(term_two, upper)
+    outs = input_grad(place, grad, before, after, kernel_two, second, width, 0)
+    term_two = kernel_term(second, True, 0)
+    term_two = fold_rows(*term_two)
     grad = outs[0]
     before, after = row_halo(outs[1], outs[2])
-    late = kernel_term(second, False, wide).astype(jnp.bfloat16)
-    late = fold_rows(late, upper)
+    late = kernel_term(second, False, wide)
+    late = fold_rows(*late)
     size = lax.axis_size("ha") // 2
     halves = [[start + i for i in range(size)] for start in (0, size)]
     terms = lax.all_to_all(
         jnp.concatenate([term_three, term_two, late], 1), "ha", 0, 0, axis_index_groups=halves, tiled=True
     )
-    own = input_grad(grad, before, after, kernel_one, None, width, 0)[0]
+    own = input_grad(place, grad, before, after, kernel_one, None, width, 0)[0]
     back = returned(own.reshape((parts, frames) + own.shape[1:]))
     back = back.reshape(layer_input.shape)
     mine = jnp.sum(terms.astype(jnp.float32), 0).reshape(3, SLOTS, channels)
-    mine = mine + swapped(mine, 2)
-    theirs = swapped(mine, 1)
+    far, across_far, near = swapped(mine, 2), swapped(mine, 3), swapped(mine, 1)
+    mine, theirs = mine + far, near + across_far
     low = jnp.where(half == 0, mine, theirs)
     high = jnp.where(half == 0, theirs, mine)
     both = jnp.stack([low, high], 2)[:, :TAPS] * norm_scale

time: 152 us -> 141 us (0.928)
  blocking collectives: 0 us -> 18.9 us
  waiting for transfers between devices: 51.1 us -> 38.1 us
  local copies, waits for them, and re-layouts: 11 us -> 0.74 us
  starting transfers between devices: 59.6 us -> 54.6 us
  other arithmetic: 4.75 us -> 2.55 us
    all_to_all x0 -> x1, blocking collectives: none -> 18.9 us  [across(): return lax.all_to_all(x, 'ta', 0, 0, tiled=True)]
    all_to_all x2 -> x0, waiting for transfers between devices: 11.2 us -> none  [across(): return lax.all_to_all(x, 'ta', 0, 0, tiled=True)]
    all_to_all x2 -> x0, starting transfers between devices: 11.2 us -> none  [across(): return lax.all_to_all(x, 'ta', 0, 0, tiled=True)]
    unnamed x46 -> x10, local copies, waits for them, and re-layouts: 10.3 us -> 0.03 us
    ppermute x8 -> x12, starting transfers between devices: 14.3 us -> 18.6 us  [swapped(): lax.ppermute(x, 'ta', [(i, i ^ bit) for i in range(lax.axis_size('ta'))])]
    all_to_all x1, starting transfers between devices: 4.99 us -> 8.21 us  [shards(): lax.all_to_all(jnp.concatenate([term_three, term_two, late], 1), 'ha', 0,...]
    ppermute x3, waiting for transfers between devices: 7.57 us -> 5.04 us  [row_halo(): after = lax.ppermute(first, 'ha', [(i + 1, i) for i in range(peers - 1)])]
    convert_element_type x3, other arithmetic: 2.58 us -> 0.2 us  [fold_rows(): send = (keep[0] + received[0].astype(jnp.float32)).astype(jnp.bfloat16)]
  transfers between devices with their start and end apart: 20 -> 22, of which waited for: 13 -> 10; matrix products, arithmetic and copies ran while one was open for 2% -> 1% of each run, Pallas kernels for 15% -> 16%
where the time goes in v2:
time: 141 us; the launch traced here: 140 us
  starting transfers between devices  54.6 us (39%)
  waiting for transfers between devices  38.1 us (27%)
  Pallas kernels  24.3 us (17%)
  blocking collectives  18.9 us (13%)
  other arithmetic  2.55 us (2%)
    pallas_call x8, Pallas kernels, call(): pl.pallas_call(kernel, out_shape=tuple(out_shape), in_specs=[SMEM] * skip...  24.3 us
    all_to_all x1, blocking collectives, across(): return lax.all_to_all(x, 'ta', 0, 0, tiled=True)  18.9 us
    ppermute x12, starting transfers between devices, swapped(): lax.ppermute(x, 'ta', [(i, i ^ bit) for i in range(lax.axis_size('ta'))])  18.6 us
    ppermute x3, waiting for transfers between devices, fold_rows(): lax.ppermute(send, 'ha', [(i, (i + size) % peers) for i in range(peers)])  15.9 us
    ppermute x3, starting transfers between devices, fold_rows(): lax.ppermute(send, 'ha', [(i, (i + size) % peers) for i in range(peers)])  12.8 us
    ppermute x3, starting transfers between devices, row_halo(): before = lax.ppermute(final, 'ha', [(i, i + 1) for i in range(peers - 1)])  11.1 us
    all_to_all x1, waiting for transfers between devices, shards(): lax.all_to_all(jnp.concatenate([term_three, term_two, late], 1), 'ha', 0,...  9.42 us
    all_to_all x1, starting transfers between devices, shards(): lax.all_to_all(jnp.concatenate([term_three, term_two, late], 1), 'ha', 0,...  8.21 us
  transfers between devices with their start and end apart: 22, of which 10 were waited for; matrix products, arithmetic and copies ran while one was open for 1% of the time, Pallas kernels for 16%

profile of v2, /device:TPU:1, one launch (start us, length us, event | category | flops | bytes accessed | tf_op | source)
XLA Modules:
  0.0 140.1 jit_solution(15794447140559278693)
XLA Ops:
  0.6 2.3 %shard_map.111 = bf16[4,2,3,128,128]{4,3,2,1,0:T(8,128)(2,1)} custom-call(bf16[2,3,192,128]{3,2,1,0:T(8,128)(2,1)} %refs_0_.1, bf16[2,3,192,128]{3,2,1,0:T(8,128)(2,1)} %refs_1_.2, bf16[2,3,192,128]{3,2,1,0:T(8,128)(2,1)} %refs_2_.2), custom_call_target="tpu_custom_call" | custom-call | flops 1000000 | bytes 1671168 | tf_op jit(solution)/shard_map/pallas_call | solution.py:50
  2.9 18.9 %all_to_all.10 = bf16[4,2,3,128,128]{4,3,2,1,0:T(8,128)(2,1)S(1)} all-to-all(bf16[4,2,3,128,128]{4,3,2,1,0:T(8,128)(2,1)} %shard_map.111), channel_id=1, replica_groups=mesh['ha'=64,'ta'=4] {'ta'}, dimensions={0} | all-to-all | bytes 1572864 | tf_op jit(solution)/shard_map/all_to_all | solution.py:263
  21.9 2.4 %collective-permute-start = (bf16[8,64,128]{2,1,0:T(8,128)(2,1)S(1)}, bf16[8,64,128]{2,1,0:T(8,128)(2,1)S(1)}, u32[]{:S(2)}, u32[]{:S(2)}) collective-permute-start(bf16[8,64,128]{2,1,0:T(8,128)(2,1)S(1)} %get-tuple-element.37), channel_id=1, source_target_pairs={{0,4},{4,8},{8,12},{12,16},{16,20},{20,24},{24,28},{28,32},{32,36}... | collective-permute-start | bytes 393224 | tf_op jit(solution)/shard_map/ppermute | solution.py:257
  24.3 1.3 collective-permute-start.1
  26.3 1.4 %collective-permute-start.4 = (bf16[2,3,112,128]{3,2,1,0:T(8,128)(2,1)S(1)}, bf16[2,3,112,128]{3,2,1,0:T(8,128)(2,1)S(1)}, u32[]{:S(2)}, u32[]{:S(2)}) collective-permute-start(bf16[2,3,112,128]{3,2,1,0:T(8,128)(2,1)S(1)} %get-tuple-element.24), channel_id=1, source_target_pairs={{0,1},{1,0},{2,3},{3,2},{4,5},{5,4},{6,7},{7,6},{8,9},{9,8},{10,11... | collective-permute-start | bytes 516104 | tf_op jit(solution)/shard_map/ppermute | solution.py:252
  27.9 3.1 %collective-permute-start.6 = (bf16[2,3,112,128]{3,2,1,0:T(8,128)(2,1)S(1)}, bf16[2,3,112,128]{3,2,1,0:T(8,128)(2,1)S(1)}, u32[]{:S(2)}, u32[]{:S(2)}) collective-permute-start(bf16[2,3,112,128]{3,2,1,0:T(8,128)(2,1)S(1)} %get-tuple-element.26), channel_id=1, source_target_pairs={{0,3},{1,2},{2,1},{3,0},{4,7},{5,6},{6,5},{7,4},{8,11},{9,10},{10,... | collective-permute-start | bytes 516104 | tf_op jit(solution)/shard_map/ppermute | solution.py:252
  31.0 3.6 %shard_map.112 = (bf16[8,3,64,128]{3,2,1,0:T(8,128)(2,1)S(1)}, bf16[8,64,128]{2,1,0:T(8,128)(2,1)S(1)}, bf16[8,64,128]{2,1,0:T(8,128)(2,1)S(1)}) custom-call(s32[3]{0:T(128)S(1)} %pad_add_fusion.refs_0_, bf16[8,3,128,128]{3,2,1,0:T(8,128)(2,1)S(1)} %bitcast.56, bf16[8,64,128]{2,1,0:T(8,128)(2,1)S(1)} %collective-permute-done.refs_2_, ...), custom_call_target="tpu_custom_call" | custom-call | flops 1358954496 | bytes 3375104 | tf_op jit(solution)/shard_map/pallas_call | solution.py:50
  34.6 4.3 %collective-permute-start.2 = (bf16[8,64,128]{2,1,0:T(8,128)(2,1)S(1)}, bf16[8,64,128]{2,1,0:T(8,128)(2,1)S(1)}, u32[]{:S(2)}, u32[]{:S(2)}) collective-permute-start(bf16[8,64,128]{2,1,0:T(8,128)(2,1)S(1)} %get-tuple-element.21), channel_id=1, source_target_pairs={{0,4},{4,8},{8,12},{12,16},{16,20},{20,24},{24,28},{28,32},{32,36}... | collective-permute-start | bytes 393224 | tf_op jit(solution)/shard_map/ppermute | solution.py:257
  38.9 1.3 collective-permute-start.3
  40.2 3.8 %shard_map.116 = (f32[2,32,32,128]{3,2,1,0:T(8,128)S(1)}, bf16[2,32,32,128]{3,2,1,0:T(8,128)(2,1)S(1)}) custom-call(s32[3]{0:T(128)S(1)} %pad_add_fusion.refs_0_, bf16[8,3,128,128]{3,2,1,0:T(8,128)(2,1)S(1)} %bitcast.58, bf16[8,64,128]{2,1,0:T(8,128)(2,1)S(1)} %collective-permute-done.refs_2_, bf16[8,64,128]{2,1,0:T(8,128)(2,1)S(1)} %collective-permute-done.1.refs_3_, ...), custom_call_target="tpu_custom_call" | custom-call | flops 1019215872 | bytes 3407872 | tf_op jit(solution)/shard_map/pallas_call | solution.py:50
  45.2 3.8 %shard_map.117 = (f32[2,32,32,128]{3,2,1,0:T(8,128)S(1)}, bf16[2,32,32,128]{3,2,1,0:T(8,128)(2,1)S(1)}) custom-call(s32[3]{0:T(128)S(1)} %pad_add_fusion.refs_0_, bf16[8,3,64,128]{3,2,1,0:T(8,128)(2,1)S(1)} %get-tuple-element.20.refs_1_, bf16[8,64,128]{2,1,0:T(8,128)(2,1)S(1)} %collective-permute-done.2.refs_2_, ...), custom_call_target="tpu_custom_call" | custom-call | flops 1019215872 | bytes 2916352 | tf_op jit(solution)/shard_map/pallas_call | solution.py:50
  49.1 1.7 %collective-permute-start.14 = (bf16[2,32,32,128]{3,2,1,0:T(8,128)(2,1)S(1)}, bf16[2,32,32,128]{3,2,1,0:T(8,128)(2,1)S(1)}, u32[]{:S(2)}, u32[]{:S(2)}) collective-permute-start(bf16[2,32,32,128]{3,2,1,0:T(8,128)(2,1)S(1)} %get-tuple-element.33), channel_id=1, source_target_pairs={{0,1},{1,0},{2,3},{3,2},{4,5},{5,4},{6,7},{7,6},{8,9},{9,8},{10,11... | collective-permute-start | bytes 1572872 | tf_op jit(solution)/shard_map/ppermute | solution.py:252
  50.8 3.6 %shard_map.114 = (bf16[8,3,64,128]{3,2,1,0:T(8,128)(2,1)S(1)}, bf16[8,64,128]{2,1,0:T(8,128)(2,1)S(1)}, bf16[8,64,128]{2,1,0:T(8,128)(2,1)S(1)}) custom-call(s32[3]{0:T(128)S(1)} %pad_add_fusion.refs_0_, bf16[8,3,64,128]{3,2,1,0:T(8,128)(2,1)S(1)} %get-tuple-element.20.refs_1_, bf16[8,64,128]{2,1,0:T(8,128)(2,1)S(1)} %collective-permute-done.2.refs_2_, ...), custom_call_target="tpu_custom_call" | custom-call | flops 1358954496 | bytes 2883584 | tf_op jit(solution)/shard_map/pallas_call | solution.py:50
  54.4 4.4 %collective-permute-start.7 = (bf16[8,64,128]{2,1,0:T(8,128)(2,1)S(1)}, bf16[8,64,128]{2,1,0:T(8,128)(2,1)S(1)}, u32[]{:S(2)}, u32[]{:S(2)}) collective-permute-start(bf16[8,64,128]{2,1,0:T(8,128)(2,1)S(1)} %get-tuple-element.28), channel_id=1, source_target_pairs={{0,4},{4,8},{8,12},{12,16},{16,20},{20,24},{24,28},{28,32},{32,36}... | collective-permute-start | bytes 393224 | tf_op jit(solution)/shard_map/ppermute | solution.py:257
  58.8 1.3 collective-permute-start.8
  60.1 1.5 %collective-permute-done.7.refs_2_ = bf16[8,64,128]{2,1,0:T(8,128)(2,1)S(1)} collective-permute-done((bf16[8,64,128]{2,1,0:T(8,128)(2,1)S(1)}, bf16[8,64,128]{2,1,0:T(8,128)(2,1)S(1)}, u32[]{:S(2)}, u32[]{:S(2)}) %collective-permute-start.7) | collective-permute-done | bytes 131104 | tf_op jit(solution)/shard_map/ppermute | solution.py:257
  61.6 4.5 %collective-permute-done.8.refs_3_ = bf16[8,64,128]{2,1,0:T(8,128)(2,1)S(1)} collective-permute-done((bf16[8,64,128]{2,1,0:T(8,128)(2,1)S(1)}, bf16[8,64,128]{2,1,0:T(8,128)(2,1)S(1)}, u32[]{:S(2)}, u32[]{:S(2)}) %collective-permute-start.8) | collective-permute-done | bytes 131104 | tf_op jit(solution)/shard_map/ppermute | solution.py:258
  66.1 3.7 %shard_map.118 = (f32[2,32,32,128]{3,2,1,0:T(8,128)S(1)}, bf16[2,32,32,128]{3,2,1,0:T(8,128)(2,1)S(1)}) custom-call(s32[3]{0:T(128)S(1)} %pad_add_fusion.refs_0_, bf16[8,3,64,128]{3,2,1,0:T(8,128)(2,1)S(1)} %get-tuple-element.27.refs_1_, bf16[8,64,128]{2,1,0:T(8,128)(2,1)S(1)} %collective-permute-done.7.refs_2_, ...), custom_call_target="tpu_custom_call" | custom-call | flops 1019215872 | bytes 2916352 | tf_op jit(solution)/shard_map/pallas_call | solution.py:50
  70.9 11.2 %collective-permute-start.13 = (bf16[32,32,128]{2,1,0:T(8,128)(2,1)S(1)}, bf16[32,32,128]{2,1,0:T(8,128)(2,1)S(1)}, u32[]{:S(2)}, u32[]{:S(2)}) collective-permute-start(bf16[32,32,128]{2,1,0:T(8,128)(2,1)S(1)} %fusion.3), channel_id=1, source_target_pairs={{0,128},{4,132},{8,136},{12,140},{16,144},{20,148},{24,152},{28,15... | collective-permute-start | bytes 786440 | tf_op jit(solution)/shard_map/ppermute | solution.py:281
  82.3 1.5 %collective-permute-start.17 = (bf16[32,32,128]{2,1,0:T(8,128)(2,1)S(1)}, bf16[32,32,128]{2,1,0:T(8,128)(2,1)S(1)}, u32[]{:S(2)}, u32[]{:S(2)}) collective-permute-start(bf16[32,32,128]{2,1,0:T(8,128)(2,1)S(1)} %fusion.5), channel_id=1, source_target_pairs={{0,128},{4,132},{8,136},{12,140},{16,144},{20,148},{24,152},{28,15... | collective-permute-start | bytes 786440 | tf_op jit(solution)/shard_map/ppermute | solution.py:281
  83.8 4.9 %collective-permute-done.13 = bf16[32,32,128]{2,1,0:T(8,128)(2,1)S(1)} collective-permute-done((bf16[32,32,128]{2,1,0:T(8,128)(2,1)S(1)}, bf16[32,32,128]{2,1,0:T(8,128)(2,1)S(1)}, u32[]{:S(2)}, u32[]{:S(2)}) %collective-permute-start.13) | collective-permute-done | bytes 262176 | tf_op jit(solution)/shard_map/ppermute | solution.py:281
  88.8 5.5 %collective-permute-done.15 = bf16[32,32,128]{2,1,0:T(8,128)(2,1)S(1)} collective-permute-done((bf16[32,32,128]{2,1,0:T(8,128)(2,1)S(1)}, bf16[32,32,128]{2,1,0:T(8,128)(2,1)S(1)}, u32[]{:S(2)}, u32[]{:S(2)}) %collective-permute-start.15) | collective-permute-done | bytes 262176 | tf_op jit(solution)/shard_map/ppermute | solution.py:281
  94.4 5.5 %collective-permute-done.17 = bf16[32,32,128]{2,1,0:T(8,128)(2,1)S(1)} collective-permute-done((bf16[32,32,128]{2,1,0:T(8,128)(2,1)S(1)}, bf16[32,32,128]{2,1,0:T(8,128)(2,1)S(1)}, u32[]{:S(2)}, u32[]{:S(2)}) %collective-permute-start.17) | collective-permute-done | bytes 262176 | tf_op jit(solution)/shard_map/ppermute | solution.py:281
  101.0 8.2 %all-to-all-start.1 = ((bf16[32,96,128]{2,1,0:T(8,128)(2,1)}), bf16[32,96,128]{2,1,0:T(8,128)(2,1)S(1)}, u32[]{:S(2)}, u32[]{:S(2)}) async-start(bf16[32,96,128]{2,1,0:T(8,128)(2,1)} %pad_maximum_fusion), calls=%async_computation.1 | async-start | bytes 1572864 | tf_op jit(solution)/shard_map/all_to_all | solution.py:336
  109.2 2.9 %shard_map.115 = bf16[8,3,48,128]{3,2,1,0:T(8,128)(2,1)S(1)} custom-call(s32[3]{0:T(128)S(1)} %pad_add_fusion.refs_0_, bf16[8,3,64,128]{3,2,1,0:T(8,128)(2,1)S(1)} %get-tuple-element.27.refs_1_, bf16[8,64,128]{2,1,0:T(8,128)(2,1)S(1)} %collective-permute-done.7.refs_2_, bf16[8,64,128]{2,1,0:T(8,128)(2,1)S(1)} %collective-permute-done.8.refs_3_, ...), custom_call_target="tpu_custom_call" | custom-call | flops 1358954496 | bytes 1835008 | tf_op jit(solution)/shard_map/pallas_call | solution.py:50
  114.0 2.6 %collective-permute-start.11 = (bf16[2,3,48,128]{3,2,1,0:T(8,128)(2,1)S(1)}, bf16[2,3,48,128]{3,2,1,0:T(8,128)(2,1)S(1)}, u32[]{:S(2)}, u32[]{:S(2)}) collective-permute-start(bf16[2,3,48,128]{3,2,1,0:T(8,128)(2,1)S(1)} %get-tuple-element.43), channel_id=1, source_target_pairs={{0,3},{1,2},{2,1},{3,0},{4,7},{5,6},{6,5},{7,4},{8,11},{9,10},{10,... | collective-permute-start | bytes 221192 | tf_op jit(solution)/shard_map/ppermute | solution.py:252
  116.6 2.0 %collective-permute-done.10 = bf16[2,3,48,128]{3,2,1,0:T(8,128)(2,1)S(1)} collective-permute-done((bf16[2,3,48,128]{3,2,1,0:T(8,128)(2,1)S(1)}, bf16[2,3,48,128]{3,2,1,0:T(8,128)(2,1)S(1)}, u32[]{:S(2)}, u32[]{:S(2)}) %collective-permute-start.10) | collective-permute-done | bytes 73760 | tf_op jit(solution)/shard_map/ppermute | solution.py:252
  118.6 2.1 %collective-permute-done.11 = bf16[2,3,48,128]{3,2,1,0:T(8,128)(2,1)S(1)} collective-permute-done((bf16[2,3,48,128]{3,2,1,0:T(8,128)(2,1)S(1)}, bf16[2,3,48,128]{3,2,1,0:T(8,128)(2,1)S(1)}, u32[]{:S(2)}, u32[]{:S(2)}) %collective-permute-start.11) | collective-permute-done | bytes 73760 | tf_op jit(solution)/shard_map/ppermute | solution.py:252
  120.9 9.4 %all-to-all-done.1 = bf16[32,96,128]{2,1,0:T(8,128)(2,1)S(1)} async-done(((bf16[32,96,128]{2,1,0:T(8,128)(2,1)}), bf16[32,96,128]{2,1,0:T(8,128)(2,1)S(1)}, u32[]{:S(2)}, u32[]{:S(2)}) %all-to-all-start.1) | async-done | bytes 786464 | tf_op jit(solution)/shard_map/all_to_all | solution.py:336
  131.1 3.2 %collective-permute-start.19 = (f32[3,32,128]{2,1,0:T(8,128)S(1)}, f32[3,32,128]{2,1,0:T(8,128)S(1)}, u32[]{:S(2)}, u32[]{:S(2)}) collective-permute-start(f32[3,32,128]{2,1,0:T(8,128)S(1)} %bitcast.65), channel_id=1, source_target_pairs={{0,1},{1,0},{2,3},{3,2},{4,5},{5,4},{6,7},{7,6},{8,9},{9,8},{10,11... | collective-permute-start | bytes 147464 | tf_op jit(solution)/shard_map/ppermute | solution.py:252
  134.3 2.2 %collective-permute-start.20 = (f32[3,32,128]{2,1,0:T(8,128)S(1)}, f32[3,32,128]{2,1,0:T(8,128)S(1)}, u32[]{:S(2)}, u32[]{:S(2)}) collective-permute-start(f32[3,32,128]{2,1,0:T(8,128)S(1)} %bitcast.66), channel_id=1, source_target_pairs={{0,3},{1,2},{2,1},{3,0},{4,7},{5,6},{6,5},{7,4},{8,11},{9,10},{10,... | collective-permute-start | bytes 147464 | tf_op jit(solution)/shard_map/ppermute | solution.py:252
  137.3 2.1 %collective-permute-done.20 = f32[3,32,128]{2,1,0:T(8,128)S(1)} collective-permute-done((f32[3,32,128]{2,1,0:T(8,128)S(1)}, f32[3,32,128]{2,1,0:T(8,128)S(1)}, u32[]{:S(2)}, u32[]{:S(2)}) %collective-permute-start.20) | collective-permute-done | bytes 49184 | tf_op jit(solution)/shard_map/ppermute | solution.py:252
  (48 shorter events, 8.9 us)
Async XLA Ops:
  2.9 22.8 %copy-start = (bf16[2,3,192,128]{3,2,1,0:T(8,128)(2,1)S(1)}, bf16[2,3,192,128]{3,2,1,0:T(8,128)(2,1)}, u32[]{:S(2)}) copy-start(bf16[2,3,192,128]{3,2,1,0:T(8,128)(2,1)} %refs_1_.3) | copy-start | bytes 884740
  2.9 22.8 %copy-start.1 = (bf16[2,3,192,128]{3,2,1,0:T(8,128)(2,1)S(1)}, bf16[2,3,192,128]{3,2,1,0:T(8,128)(2,1)}, u32[]{:S(2)}) copy-start(bf16[2,3,192,128]{3,2,1,0:T(8,128)(2,1)} %refs_2_.3) | copy-start | bytes 884740
  2.9 28.1 %copy-start.2 = (bf16[3,3,3,128,128]{4,3,2,1,0:T(8,128)(2,1)S(1)}, bf16[3,3,3,128,128]{4,3,2,1,0:T(8,128)(2,1)}, u32[]{:S(2)}) copy-start(bf16[3,3,3,128,128]{4,3,2,1,0:T(8,128)(2,1)} %param.14) | copy-start | bytes 2654212
  21.9 9.1 %collective-permute-start = (bf16[8,64,128]{2,1,0:T(8,128)(2,1)S(1)}, bf16[8,64,128]{2,1,0:T(8,128)(2,1)S(1)}, u32[]{:S(2)}, u32[]{:S(2)}) collective-permute-start(bf16[8,64,128]{2,1,0:T(8,128)(2,1)S(1)} %get-tuple-element.37), channel_id=1, source_target_pairs={{0,4},{4,8},{8,12},{12,16},{16,20},{20,24},{24,28},{28,32},{32,36}... | collective-permute-start | bytes 393224 | tf_op jit(solution)/shard_map/ppermute | solution.py:257
  24.3 6.7 %collective-permute-start.1 = (bf16[8,64,128]{2,1,0:T(8,128)(2,1)S(1)}, bf16[8,64,128]{2,1,0:T(8,128)(2,1)S(1)}, u32[]{:S(2)}, u32[]{:S(2)}) collective-permute-start(bf16[8,64,128]{2,1,0:T(8,128)(2,1)S(1)} %get-tuple-element.36), channel_id=1, source_target_pairs={{4,0},{8,4},{12,8},{16,12},{20,16},{24,20},{28,24},{32,28},{36,32}... | collective-permute-start | bytes 393224 | tf_op jit(solution)/shard_map/ppermute | solution.py:258
  26.3 17.7 %collective-permute-start.4 = (bf16[2,3,112,128]{3,2,1,0:T(8,128)(2,1)S(1)}, bf16[2,3,112,128]{3,2,1,0:T(8,128)(2,1)S(1)}, u32[]{:S(2)}, u32[]{:S(2)}) collective-permute-start(bf16[2,3,112,128]{3,2,1,0:T(8,128)(2,1)S(1)} %get-tuple-element.24), channel_id=1, source_target_pairs={{0,1},{1,0},{2,3},{3,2},{4,5},{5,4},{6,7},{7,6},{8,9},{9,8},{10,11... | collective-permute-start | bytes 516104 | tf_op jit(solution)/shard_map/ppermute | solution.py:252
  27.7 16.9 %collective-permute-start.5 = (bf16[2,3,112,128]{3,2,1,0:T(8,128)(2,1)S(1)}, bf16[2,3,112,128]{3,2,1,0:T(8,128)(2,1)S(1)}, u32[]{:S(2)}, u32[]{:S(2)}) collective-permute-start(bf16[2,3,112,128]{3,2,1,0:T(8,128)(2,1)S(1)} %get-tuple-element.25), channel_id=1, source_target_pairs={{0,2},{1,3},{2,0},{3,1},{4,6},{5,7},{6,4},{7,5},{8,10},{9,11},{10,... | collective-permute-start | bytes 516104 | tf_op jit(solution)/shard_map/ppermute | solution.py:252
  27.9 16.8 %collective-permute-start.6 = (bf16[2,3,112,128]{3,2,1,0:T(8,128)(2,1)S(1)}, bf16[2,3,112,128]{3,2,1,0:T(8,128)(2,1)S(1)}, u32[]{:S(2)}, u32[]{:S(2)}) collective-permute-start(bf16[2,3,112,128]{3,2,1,0:T(8,128)(2,1)S(1)} %get-tuple-element.26), channel_id=1, source_target_pairs={{0,3},{1,2},{2,1},{3,0},{4,7},{5,6},{6,5},{7,4},{8,11},{9,10},{10,... | collective-permute-start | bytes 516104 | tf_op jit(solution)/shard_map/ppermute | solution.py:252
  34.6 10.1 %collective-permute-start.2 = (bf16[8,64,128]{2,1,0:T(8,128)(2,1)S(1)}, bf16[8,64,128]{2,1,0:T(8,128)(2,1)S(1)}, u32[]{:S(2)}, u32[]{:S(2)}) collective-permute-start(bf16[8,64,128]{2,1,0:T(8,128)(2,1)S(1)} %get-tuple-element.21), channel_id=1, source_target_pairs={{0,4},{4,8},{8,12},{12,16},{16,20},{20,24},{24,28},{28,32},{32,36}... | collective-permute-start | bytes 393224 | tf_op jit(solution)/shard_map/ppermute | solution.py:257
  38.9 6.4 %collective-permute-start.3 = (bf16[8,64,128]{2,1,0:T(8,128)(2,1)S(1)}, bf16[8,64,128]{2,1,0:T(8,128)(2,1)S(1)}, u32[]{:S(2)}, u32[]{:S(2)}) collective-permute-start(bf16[8,64,128]{2,1,0:T(8,128)(2,1)S(1)} %get-tuple-element.22), channel_id=1, source_target_pairs={{4,0},{8,4},{12,8},{16,12},{20,16},{24,20},{28,24},{32,28},{36,32}... | collective-permute-start | bytes 393224 | tf_op jit(solution)/shard_map/ppermute | solution.py:258
  44.0 26.8 %collective-permute-start.12 = (bf16[2,32,32,128]{3,2,1,0:T(8,128)(2,1)S(1)}, bf16[2,32,32,128]{3,2,1,0:T(8,128)(2,1)S(1)}, u32[]{:S(2)}, u32[]{:S(2)}) collective-permute-start(bf16[2,32,32,128]{3,2,1,0:T(8,128)(2,1)S(1)} %get-tuple-element.31), channel_id=1, source_target_pairs={{0,1},{1,0},{2,3},{3,2},{4,5},{5,4},{6,7},{7,6},{8,9},{9,8},{10,11... | collective-permute-start | bytes 1572872 | tf_op jit(solution)/shard_map/ppermute | solution.py:252
  45.2 5.6 %copy-start.3 = (bf16[3,3,3,128,128]{4,3,2,1,0:T(8,128)(2,1)S(1)}, bf16[3,3,3,128,128]{4,3,2,1,0:T(8,128)(2,1)}, u32[]{:S(2)}) copy-start(bf16[3,3,3,128,128]{4,3,2,1,0:T(8,128)(2,1)} %param.13) | copy-start | bytes 2654212
  49.1 33.0 %collective-permute-start.14 = (bf16[2,32,32,128]{3,2,1,0:T(8,128)(2,1)S(1)}, bf16[2,32,32,128]{3,2,1,0:T(8,128)(2,1)S(1)}, u32[]{:S(2)}, u32[]{:S(2)}) collective-permute-start(bf16[2,32,32,128]{3,2,1,0:T(8,128)(2,1)S(1)} %get-tuple-element.33), channel_id=1, source_target_pairs={{0,1},{1,0},{2,3},{3,2},{4,5},{5,4},{6,7},{7,6},{8,9},{9,8},{10,11... | collective-permute-start | bytes 1572872 | tf_op jit(solution)/shard_map/ppermute | solution.py:252
  54.4 7.2 %collective-permute-start.7 = (bf16[8,64,128]{2,1,0:T(8,128)(2,1)S(1)}, bf16[8,64,128]{2,1,0:T(8,128)(2,1)S(1)}, u32[]{:S(2)}, u32[]{:S(2)}) collective-permute-start(bf16[8,64,128]{2,1,0:T(8,128)(2,1)S(1)} %get-tuple-element.28), channel_id=1, source_target_pairs={{0,4},{4,8},{8,12},{12,16},{16,20},{20,24},{24,28},{28,32},{32,36}... | collective-permute-start | bytes 393224 | tf_op jit(solution)/shard_map/ppermute | solution.py:257
  58.8 7.3 %collective-permute-start.8 = (bf16[8,64,128]{2,1,0:T(8,128)(2,1)S(1)}, bf16[8,64,128]{2,1,0:T(8,128)(2,1)S(1)}, u32[]{:S(2)}, u32[]{:S(2)}) collective-permute-start(bf16[8,64,128]{2,1,0:T(8,128)(2,1)S(1)} %get-tuple-element.29), channel_id=1, source_target_pairs={{4,0},{8,4},{12,8},{16,12},{20,16},{24,20},{28,24},{32,28},{36,32}... | collective-permute-start | bytes 393224 | tf_op jit(solution)/shard_map/ppermute | solution.py:258
  69.8 12.4 %collective-permute-start.16 = (bf16[2,32,32,128]{3,2,1,0:T(8,128)(2,1)S(1)}, bf16[2,32,32,128]{3,2,1,0:T(8,128)(2,1)S(1)}, u32[]{:S(2)}, u32[]{:S(2)}) collective-permute-start(bf16[2,32,32,128]{3,2,1,0:T(8,128)(2,1)S(1)} %get-tuple-element.35), channel_id=1, source_target_pairs={{0,1},{1,0},{2,3},{3,2},{4,5},{5,4},{6,7},{7,6},{8,9},{9,8},{10,11... | collective-permute-start | bytes 1572872 | tf_op jit(solution)/shard_map/ppermute | solution.py:252
  70.9 17.8 %collective-permute-start.13 = (bf16[32,32,128]{2,1,0:T(8,128)(2,1)S(1)}, bf16[32,32,128]{2,1,0:T(8,128)(2,1)S(1)}, u32[]{:S(2)}, u32[]{:S(2)}) collective-permute-start(bf16[32,32,128]{2,1,0:T(8,128)(2,1)S(1)} %fusion.3), channel_id=1, source_target_pairs={{0,128},{4,132},{8,136},{12,140},{16,144},{20,148},{24,152},{28,15... | collective-permute-start | bytes 786440 | tf_op jit(solution)/shard_map/ppermute | solution.py:281
  82.1 12.2 %collective-permute-start.15 = (bf16[32,32,128]{2,1,0:T(8,128)(2,1)S(1)}, bf16[32,32,128]{2,1,0:T(8,128)(2,1)S(1)}, u32[]{:S(2)}, u32[]{:S(2)}) collective-permute-start(bf16[32,32,128]{2,1,0:T(8,128)(2,1)S(1)} %fusion.4), channel_id=1, source_target_pairs={{0,128},{4,132},{8,136},{12,140},{16,144},{20,148},{24,152},{28,15... | collective-permute-start | bytes 786440 | tf_op jit(solution)/shard_map/ppermute | solution.py:281
  82.3 17.6 %collective-permute-start.17 = (bf16[32,32,128]{2,1,0:T(8,128)(2,1)S(1)}, bf16[32,32,128]{2,1,0:T(8,128)(2,1)S(1)}, u32[]{:S(2)}, u32[]{:S(2)}) collective-permute-start(bf16[32,32,128]{2,1,0:T(8,128)(2,1)S(1)} %fusion.5), channel_id=1, source_target_pairs={{0,128},{4,132},{8,136},{12,140},{16,144},{20,148},{24,152},{28,15... | collective-permute-start | bytes 786440 | tf_op jit(solution)/shard_map/ppermute | solution.py:281
  101.0 8.2 %copy-start.4 = (bf16[3,3,3,128,128]{4,3,2,1,0:T(8,128)(2,1)S(1)}, bf16[3,3,3,128,128]{4,3,2,1,0:T(8,128)(2,1)}, u32[]{:S(2)}) copy-start(bf16[3,3,3,128,128]{4,3,2,1,0:T(8,128)(2,1)} %param.12) | copy-start | bytes 2654212
  101.0 29.3 %all-to-all-start.1 = ((bf16[32,96,128]{2,1,0:T(8,128)(2,1)}), bf16[32,96,128]{2,1,0:T(8,128)(2,1)S(1)}, u32[]{:S(2)}, u32[]{:S(2)}) async-start(bf16[32,96,128]{2,1,0:T(8,128)(2,1)} %pad_maximum_fusion), calls=%async_computation.1 | async-start | bytes 1572864 | tf_op jit(solution)/shard_map/all_to_all | solution.py:336
  112.2 4.5 %collective-permute-start.9 = (bf16[2,3,48,128]{3,2,1,0:T(8,128)(2,1)S(1)}, bf16[2,3,48,128]{3,2,1,0:T(8,128)(2,1)S(1)}, u32[]{:S(2)}, u32[]{:S(2)}) collective-permute-start(bf16[2,3,48,128]{3,2,1,0:T(8,128)(2,1)S(1)} %get-tuple-element.45), channel_id=1, source_target_pairs={{0,1},{1,0},{2,3},{3,2},{4,5},{5,4},{6,7},{7,6},{8,9},{9,8},{10,11... | collective-permute-start | bytes 221192 | tf_op jit(solution)/shard_map/ppermute | solution.py:252
  113.4 5.2 %collective-permute-start.10 = (bf16[2,3,48,128]{3,2,1,0:T(8,128)(2,1)S(1)}, bf16[2,3,48,128]{3,2,1,0:T(8,128)(2,1)S(1)}, u32[]{:S(2)}, u32[]{:S(2)}) collective-permute-start(bf16[2,3,48,128]{3,2,1,0:T(8,128)(2,1)S(1)} %get-tuple-element.44), channel_id=1, source_target_pairs={{0,2},{1,3},{2,0},{3,1},{4,6},{5,7},{6,4},{7,5},{8,10},{9,11},{10,... | collective-permute-start | bytes 221192 | tf_op jit(solution)/shard_map/ppermute | solution.py:252
  114.0 6.8 %collective-permute-start.11 = (bf16[2,3,48,128]{3,2,1,0:T(8,128)(2,1)S(1)}, bf16[2,3,48,128]{3,2,1,0:T(8,128)(2,1)S(1)}, u32[]{:S(2)}, u32[]{:S(2)}) collective-permute-start(bf16[2,3,48,128]{3,2,1,0:T(8,128)(2,1)S(1)} %get-tuple-element.43), channel_id=1, source_target_pairs={{0,3},{1,2},{2,1},{3,0},{4,7},{5,6},{6,5},{7,4},{8,11},{9,10},{10,... | collective-permute-start | bytes 221192 | tf_op jit(solution)/shard_map/ppermute | solution.py:252
  130.4 6.8 %collective-permute-start.18 = (f32[3,32,128]{2,1,0:T(8,128)S(1)}, f32[3,32,128]{2,1,0:T(8,128)S(1)}, u32[]{:S(2)}, u32[]{:S(2)}) collective-permute-start(f32[3,32,128]{2,1,0:T(8,128)S(1)} %bitcast.64), channel_id=1, source_target_pairs={{0,2},{1,3},{2,0},{3,1},{4,6},{5,7},{6,4},{7,5},{8,10},{9,11},{10,... | collective-permute-start | bytes 147464 | tf_op jit(solution)/shard_map/ppermute | solution.py:252
  131.1 6.2 %collective-permute-start.19 = (f32[3,32,128]{2,1,0:T(8,128)S(1)}, f32[3,32,128]{2,1,0:T(8,128)S(1)}, u32[]{:S(2)}, u32[]{:S(2)}) collective-permute-start(f32[3,32,128]{2,1,0:T(8,128)S(1)} %bitcast.65), channel_id=1, source_target_pairs={{0,1},{1,0},{2,3},{3,2},{4,5},{5,4},{6,7},{7,6},{8,9},{9,8},{10,11... | collective-permute-start | bytes 147464 | tf_op jit(solution)/shard_map/ppermute | solution.py:252
  134.3 5.1 %collective-permute-start.20 = (f32[3,32,128]{2,1,0:T(8,128)S(1)}, f32[3,32,128]{2,1,0:T(8,128)S(1)}, u32[]{:S(2)}, u32[]{:S(2)}) collective-permute-start(f32[3,32,128]{2,1,0:T(8,128)S(1)} %bitcast.66), channel_id=1, source_target_pairs={{0,3},{1,2},{2,1},{3,0},{4,7},{5,6},{6,5},{7,4},{8,11},{9,10},{10,... | collective-permute-start | bytes 147464 | tf_op jit(solution)/shard_map/ppermute | solution.py:252
